TPU v7x, 32 devices: a whole 2x2x4 slice. The times are simulated.
32 devices in a mesh: dp: 2 (over y), mp: 16 (over z, x, core).
Axes of the slice: x: 2, y: 2, z: 4, core: 2. Of those that a mesh axis runs over, the one named last changes fastest.
Arguments:
- features: bfloat16 [32, 1280, 1024], P('dp', 'mp'), may hold values from -6 to 6
- conv_weight: bfloat16 [1280, 1280], P('mp'), may hold values from -0.15625 to 0.15625
- norm_gain: float32 [1280], replicated, may hold values from 0.25 to 1.75
- norm_bias: float32 [1280], replicated, may hold values from -3 to 3
- logit_vector: float32 [1280], replicated, may hold values from -0.625 to 0.625
- labels: int32 [32], P(('dp', 'mp')), may hold values 0 or 1
Outputs:
- grad_features: float32 [32, 1280, 1024], P('dp', 'mp')
- grad_weight: float32 [1280, 1280], P('mp')
- head_grads: float32 [3, 1280], replicated
- loss: float32 [], replicated
All inputs are finite; a program needn't handle non-finite values. No bound on the sum of `labels` on one device may be relied on, other than what follows from the above.
Results may differ from a plain program's by a relative error of at most 0.0029.
Values may be sent and summed in bfloat16 or wider, within the bound.
No kernel may reach another device: no remote copies, remote signals or barrier semaphores. Data moves between devices by JAX's collectives and lax.ppermute only.
A program may use at most 128 MiB of HBM per device.

v0:
```python
import jax
import jax.numpy as jnp
from jax import lax
from jax.sharding import PartitionSpec as P

GROUPS = 32


norm_eps = 1e-05


def head_total(pre, norm_gain, norm_bias, logit_vector, signs):
    images, channels, cell_count = pre.shape
    grouped = pre.reshape(images, GROUPS, channels // GROUPS, cell_count)
    center = jnp.mean(grouped, axis=(2, 3), keepdims=True)
    spread = jnp.mean((grouped - center) ** 2, axis=(2, 3), keepdims=True)
    normed = ((grouped - center) * lax.rsqrt(spread + norm_eps)).reshape(
        images, channels, cell_count
    )
    normed = normed * norm_gain[:, None] + norm_bias[:, None]
    hidden = jax.nn.silu(normed)
    logits = (
        jnp.einsum("c,ncs->n", logit_vector, hidden, precision=lax.Precision.HIGHEST) / cell_count
    )
    margin = jnp.maximum(1.0 - signs * logits, 0.0)
    return jnp.sum(margin * margin)


def shards(features, conv_weight, norm_gain, norm_bias, logit_vector, labels):
    signs = 2.0 * labels.astype(jnp.float32) - 1.0
    weight_full = lax.all_gather(conv_weight, "mp", axis=0, tiled=True)
    image_block = lax.all_to_all(features, "mp", split_axis=0, concat_axis=1, tiled=True)
    pre = jnp.einsum("io,nis->nos", weight_full, image_block, preferred_element_type=jnp.float32)
    total, pull = jax.vjp(
        lambda p, g, b, h: head_total(p, g, b, h, signs), pre, norm_gain, norm_bias, logit_vector
    )
    grad_pre, grad_gain, grad_bias, grad_vec = pull(jnp.ones((), jnp.float32))
    grad_pre = grad_pre.astype(jnp.bfloat16)
    grad_image = jnp.einsum(
        "io,nos->nis", weight_full, grad_pre, preferred_element_type=jnp.float32
    )
    grad_features = lax.all_to_all(grad_image, "mp", split_axis=1, concat_axis=0, tiled=True)
    weight_term = jnp.einsum(
        "nis,nos->io", image_block, grad_pre, preferred_element_type=jnp.float32
    )
    summed = lax.psum(weight_term, "dp")
    grad_weight = lax.psum_scatter(summed, "mp", scatter_dimension=0, tiled=True)
    total_sum, head_grads = lax.psum(
        (total, jnp.stack([grad_gain, grad_bias, grad_vec])), ("dp", "mp")
    )
    image_total = pre.shape[0] * lax.axis_size("dp") * lax.axis_size("mp")
    loss = total_sum / image_total
    return (grad_features, grad_weight, head_grads, loss)


def solution(mesh):
    return jax.shard_map(
        shards,
        mesh=mesh,
        in_specs=(P("dp", "mp", None), P("mp", None), P(), P(), P(), P(("dp", "mp"))),
        out_specs=(P("dp", "mp", None), P("mp", None), P(), P()),
        check_vma=False,
    )
```

profile of v0, /device:TPU:12, one launch (start us, length us, event | category | flops | bytes accessed | tf_op | source)
XLA Modules:
  0.0 369.9 jit_solution(1314709763259043762)
XLA Ops:
  7.2 0.7 all-gather.2.cloned.1.call-update
  7.9 6.3 %all-to-all-start = ((bf16[16,80,1024]{2,1,0:T(8,128)(2,1)}), bf16[16,80,1024]{2,1,0:T(8,128)(2,1)S(1)}, u32[]{:S(2)}, u32[]{:S(2)}) async-start(bf16[16,80,1024]{2,1,0:T(8,128)(2,1)} %param.6), calls=%async_computation | async-start | bytes 5242880 | tf_op jit(solution)/shard_map/all_to_all | solution.py:32
  14.9 76.1 %all-to-all-done = bf16[16,80,1024]{2,1,0:T(8,128)(2,1)S(1)} async-done(((bf16[16,80,1024]{2,1,0:T(8,128)(2,1)}), bf16[16,80,1024]{2,1,0:T(8,128)(2,1)S(1)}, u32[]{:S(2)}, u32[]{:S(2)}) %all-to-all-start) | async-done | bytes 2621472 | tf_op jit(solution)/shard_map/all_to_all | solution.py:32
  91.0 7.3 %fusion.10 = (f32[1280]{0:T(1024)S(1)}, f32[1024,1280]{1,0:T(8,128)}) fusion(bf16[1280,1024]{1,0:T(8,128)(2,1)S(1)} %bitcast.86, bf16[1280,1280]{1,0:T(8,128)(2,1)} %all-gather.2.cloned.1.call-done), kind=kOutput, calls=%fused_computation.30 | convolution fusion | flops 3356752640 | bytes 11146240 | tf_op jit(solution)/shard_map/io,nis->nos/dot_general | solution.py:33
  98.4 0.1 reduce_sum.139
  98.6 0.1 sub.53
  98.7 3.1 fusion.2
  101.8 0.1 reduce_sum.141
  101.9 0.1 reduce_sum.142
  102.1 0.1 mul.156
  102.2 4.2 %multiply_reduce_fusion.1 = f32[1280]{0:T(1024)S(1)} fusion(f32[1024,1280]{1,0:T(8,128)} %get-tuple-element.27, f32[1280]{0:T(1024)S(1)} %copy-done, f32[1280]{0:T(1024)S(1)} %copy-done.1, f32[1280]{0:T(1024)S(1)} %mul.156, f32[1280]{0:T(1024)S(1)} %sub.53), kind=kLoop, calls=%fused_computation.13 | loop fusion | flops 11795200 | bytes 5268480 | tf_op jit(solution)/shard_map/jvp(c,ncs->n)/reduce_sum | solution.py:23
  106.4 0.6 multiply_reduce_fusion.3
  107.7 5.7 %multiply_reduce_fusion = (f32[1280]{0:T(1024)S(1)}, f32[1280]{0:T(1024)S(1)}, f32[1280]{0:T(1024)S(1)}, f32[1280]{0:T(1024)S(1)}) fusion(f32[1024,1280]{1,0:T(8,128)} %get-tuple-element.27, f32[1280]{0:T(1024)S(1)} %mul.156, f32[1280]{0:T(1024)S(1)} %sub.53, f32[1280]{0:T(1024)S(1)} %copy-done, f32[1280]{0:T(1024)S(1)} %copy-done.1, ...), kind=kLoop, calls=%fused_computation.11 | loop fusion | flops 27520000 | bytes 5288960 | tf_op jit(solution)/shard_map/transpose(jvp())/reduce_sum | solution.py:20
  113.4 0.1 reduce_sum.148
  113.5 0.1 reduce_sum.149
  113.6 0.1 reduce_sum.145
  113.7 0.1 reduce_sum.146
  113.9 0.1 mul.178
  114.0 3.1 fusion.4
  117.1 0.1 reduce_sum.151
  117.2 0.1 reduce_sum.152
  117.4 0.1 broadcast_in_dim.10
  117.5 11.6 %convolution_bitcast_fusion = f32[1280,1280]{0,1:T(8,128)} fusion(bf16[1280,1024]{1,0:T(8,128)(2,1)S(1)} %bitcast.87, f32[1024,1280]{1,0:T(8,128)} %get-tuple-element.27, f32[1280]{0:T(1024)S(1)} %broadcast_in_dim.10, f32[1280]{0:T(1024)S(1)} %mul.178, f32[1280]{0:T(1024)S(1)} %copy-done.1, f32[1280]{0:T(1024)S(1)} %mul.156, f32[1280]{0:T(1024)S(1)} %sub.53, ...), kind=kOutput, calls=%fused_computation | convolution fusion | flops 3380346880 | bytes 14453760 | tf_op jit(solution)/shard_map/nis,nos->io/dot_general | solution.py:43
  129.1 8.2 %copy.20 = f32[1280,1280]{1,0:T(8,128)} copy(f32[1280,1280]{0,1:T(8,128)} %convolution_bitcast_fusion) | data formatting | bytes 13107200
  137.3 12.1 %convolution_bitcast_fusion.1 = f32[1,1280,1024]{1,2,0:T(8,128)} fusion(bf16[1280,1280]{1,0:T(8,128)(2,1)} %all-gather.2.cloned.1.call-done, f32[1024,1280]{1,0:T(8,128)} %get-tuple-element.27, f32[1280]{0:T(1024)S(1)} %broadcast_in_dim.10, f32[1280]{0:T(1024)S(1)} %mul.178, f32[1280]{0:T(1024)S(1)} %copy-done.1, f32[1280]{0:T(1024)S(1)} %mul.156, ...), kind=kOutput, calls=%fused_computation.18 | convolution fusion | flops 3380346880 | bytes 13798400 | tf_op jit(solution)/shard_map/io,nos->nis/dot_general | solution.py:39
  149.4 11.9 %copy.16 = f32[1,1280,1024]{2,0,1:T(1,128)} copy(f32[1,1280,1024]{1,2,0:T(8,128)} %convolution_bitcast_fusion.1) | data formatting | bytes 10485760 | tf_op jit(solution)/shard_map/io,nos->nis/transpose | solution.py:39
  161.3 6.4 %all-to-all-start.1 = ((f32[1,1280,1024]{2,0,1:T(1,128)}), f32[1,1280,1024]{2,0,1:T(1,128)}, u32[]{:S(2)}, u32[]{:S(2)}) async-start(f32[1,1280,1024]{2,0,1:T(1,128)} %copy.16), calls=%async_computation.1 | async-start | bytes 10485760 | tf_op jit(solution)/shard_map/all_to_all | solution.py:42
  167.7 133.2 %reduce-scatter.4.cloned.1.call-done = f32[80,1280]{1,0:T(8,128)} async-done(((f32[1280,1280]{1,0:T(8,128)}), f32[80,1280]{1,0:T(8,128)}) %reduce-scatter.4.cloned.1.call-update) | async-done | bytes 409616
  300.9 2.1 copy.21
  303.1 50.3 %all-reduce = (f32[3,1280]{1,0:T(4,128)}, f32[]{:T(128)}) all-reduce(f32[3,1280]{1,0:T(4,128)S(1)} %pad_maximum_fusion, f32[]{:T(128)} %bitcast.9), channel_id=1, replica_groups=mesh['dp'=2,'mp'=16] {'dp','mp'}, use_global_device_ids=true, to_apply=%region_15.16 | all-reduce | flops 3841 | bytes 30728 | tf_op jit(solution)/shard_map/psum | solution.py:48
  354.0 6.1 %copy.22 = f32[1,1280,1024]{2,1,0:T(8,128)} copy(f32[1,1280,1024]{2,0,1:T(1,128)} %all-to-all-done.1) | data formatting | bytes 10485760
  360.2 2.1 copy.17
  (29 shorter events, 0.6 us)
Async XLA Ops:
  7.2 83.9 %all-gather.2.cloned.1.call-start = ((), (), s32[]{:S(2)}) async-start(), calls=%async_computation.3 | async-start | bytes 3481600 | tf_op jit(solution)/shard_map/all_gather | solution.py:31
  7.9 83.1 %all-to-all-start = ((bf16[16,80,1024]{2,1,0:T(8,128)(2,1)}), bf16[16,80,1024]{2,1,0:T(8,128)(2,1)S(1)}, u32[]{:S(2)}, u32[]{:S(2)}) async-start(bf16[16,80,1024]{2,1,0:T(8,128)(2,1)} %param.6), calls=%async_computation | async-start | bytes 5242880 | tf_op jit(solution)/shard_map/all_to_all | solution.py:32
  14.2 286.7 %reduce-scatter.4.cloned.1.call-start = ((), (), s32[]{:S(2)}) async-start(), calls=%async_computation.5 | async-start | bytes 6963200
  98.3 3.9 %copy-start = (f32[1280]{0:T(1024)S(1)}, f32[1280]{0:T(1024)}, u32[]{:S(2)}) copy-start(f32[1280]{0:T(1024)} %param.9) | copy-start | bytes 15364
  98.3 3.9 %copy-start.1 = (f32[1280]{0:T(1024)S(1)}, f32[1280]{0:T(1024)}, u32[]{:S(2)}) copy-start(f32[1280]{0:T(1024)} %param.8) | copy-start | bytes 15364
  98.7 7.7 %copy-start.2 = (f32[1280]{0:T(1024)S(1)}, f32[1280]{0:T(1024)}, u32[]{:S(2)}) copy-start(f32[1280]{0:T(1024)} %param.10) | copy-start | bytes 15364
  161.3 192.7 %all-to-all-start.1 = ((f32[1,1280,1024]{2,0,1:T(1,128)}), f32[1,1280,1024]{2,0,1:T(1,128)}, u32[]{:S(2)}, u32[]{:S(2)}) async-start(f32[1,1280,1024]{2,0,1:T(1,128)} %copy.16), calls=%async_computation.1 | async-start | bytes 10485760 | tf_op jit(solution)/shard_map/all_to_all | solution.py:42
  167.7 192.5 %all-reduce.3.cloned.1.call-start = ((), (), s32[]{:S(2)}) async-start(), calls=%async_computation.4 | async-start | bytes 1310720 | tf_op jit(solution)/shard_map/psum | solution.py:46
Sparse Core Ops, SparseCore 0:
  10.3 75.0 all-gather.1
  137.4 163.3 reduce-scatter.3
  303.2 30.7 all-reduce.2
where the time goes:
time: 371 us; the launch traced here: 370 us
  waiting for transfers between devices  210 us (57%)
  blocking collectives  50.3 us (14%)
  local copies, waits for them, and re-layouts  31.4 us (8%)
  matrix products  31.1 us (8%)
  other arithmetic  17.3 us (5%)
  between operations  17 us (5%)
  starting transfers between devices  12.8 us (3%)
    unnamed x4, waiting for transfers between devices  134 us
    all_to_all x1, waiting for transfers between devices, shards(): lax.all_to_all(features, 'mp', split_axis=0, concat_axis=1, tiled=True)  76.1 us
    psum x1, blocking collectives, shards(): lax.psum((total, jnp.stack([grad_gain, grad_bias, grad_vec])), ('dp', 'mp'))  50.3 us
    unnamed x10, local copies, waits for them, and re-layouts  18.4 us
    dot_general x1, matrix products, shards(): jnp.einsum('io,nos->nis', weight_full, grad_pre, preferred_element_type=j...  12.1 us
    transpose x1, local copies, waits for them, and re-layouts, shards(): jnp.einsum('io,nos->nis', weight_full, grad_pre, preferred_element_type=j...  11.9 us
    dot_general x1, matrix products, shards(): jnp.einsum('nis,nos->io', image_block, grad_pre, preferred_element_type=j...  11.6 us
  transfers between devices with their start and end apart: 5, of which 2 were waited for; matrix products, arithmetic and copies ran while one was open for 9% of the time, Pallas kernels for 0%

commit v1 on v0

--- a/solution.py
+++ b/solution.py
@@ -1,12 +1,462 @@
+import functools
+
 import jax
 import jax.numpy as jnp
 from jax import lax
+from jax.experimental import pallas as pl
+from jax.experimental.pallas import tpu as pltpu
 from jax.sharding import PartitionSpec as P
 
 GROUPS = 32
-
-
 norm_eps = 1e-05
+F32 = jnp.float32
+BF16 = jnp.bfloat16
+VMEM = pl.BlockSpec(memory_space=pltpu.VMEM)
+SMEM = pl.BlockSpec(memory_space=pltpu.SMEM)
+EXTRA = 8
+
+
+def stacked(refs):
+    return jnp.concatenate([ref[...] for ref in refs])
+
+
+def weight_columns(rows, grad_pre, out):
+    ch = grad_pre.shape[0]
+    step = ch // 5
+    for j in range(5):
+        cols = pl.ds(j * step, step)
+        out[: rows.shape[0], cols] = lax.dot_general(
+            rows, grad_pre[cols, :], (((1,), (1,)), ((), ())), preferred_element_type=F32
+        )
+
+
+def head_kernel(
+    info_ref, begun_ref, turned_ref, par_ref, *refs,
+):
+    last_refs, refs = refs[:4], refs[4:]
+    pre_grad_ref, small_ref, pre_ref, slope_ref, sums_ref, center_ref, rstd_ref = refs
+    ch, cells = pre_ref.shape
+    width = ch // GROUPS
+    count = width * cells
+    add_product(begun_ref, turned_ref, last_refs, pre_ref)
+
+    def at(g):
+        return pl.ds(pl.multiple_of(g * width, 8), width)
+
+    def tile(g, r):
+        return pl.ds(pl.multiple_of(g * width + 8 * r, 8), 8)
+
+    tiles, lanes = range(width // 8), [pl.ds(128 * c, 128) for c in range(cells // 128)]
+
+    def sweep(body, trips, unroll):
+        lax.fori_loop(0, trips, lambda g, _: body(g) or 0, 0, unroll=unroll)
+
+    def spot(value):
+        return jnp.broadcast_to(value, (8, 128))
+
+    def means(g):
+        center_ref[g] = spot(jnp.sum(pre_ref[at(g), :], axis=(0, 1), keepdims=True) / count)
+
+    def spreads(g):
+        center, acc = center_ref[g], jnp.zeros((8, 128), F32)
+        for r in tiles:
+            for c in lanes:
+                dev = pre_ref[tile(g, r), c] - center
+                acc += dev * dev
+        spread = jnp.sum(acc, axis=(0, 1), keepdims=True) / count
+        rstd_ref[g] = spot(lax.rsqrt(spread + norm_eps))
+
+    def activate(g):
+        center, rstd = center_ref[g], rstd_ref[g]
+        for r in tiles:
+            rows = tile(g, r)
+            a, b = par_ref[0, rows, :] * (0.5 * rstd), 0.5 * par_ref[1, rows, :]
+            sum_h = sum_d = sum_du = jnp.zeros((8, 128), F32)
+            for c in lanes:
+                dev = pre_ref[rows, c] - center
+                w = dev * a + b
+                t = jnp.tanh(w)
+                q = 1.0 + t
+                h = w * q
+                d2 = q + h * (1.0 - t)
+                slope_ref[rows, c] = d2
+                sum_h += h
+                sum_d += d2
+                sum_du += d2 * dev
+            sums_ref[0, rows, :] = sum_du * (0.5 * rstd)
+            sums_ref[1, rows, :] = 0.5 * sum_d
+            sums_ref[2, rows, :] = sum_h
+
+    sweep(means, GROUPS, 8)
+    sweep(spreads, GROUPS, 8)
+    sweep(activate, GROUPS, 2)
+
+    def total(g):
+        for i in range(3):
+            lane_sum = jnp.sum(sums_ref[i, at(g), :], axis=1, keepdims=True)
+            sums_ref[i, at(g), :] = jnp.broadcast_to(lane_sum, (width, 128))
+
+    sweep(total, GROUPS, 8)
+    logit = jnp.sum(par_ref[2] * sums_ref[2], axis=0, keepdims=True) / cells
+    sign = info_ref[0].astype(F32)
+    margin = jnp.maximum(1.0 - sign * logit, 0.0)
+    k = (-2.0 * sign / cells) * margin
+
+    def finish(pair):
+        out = {}
+        for side in range(2):
+            g = 2 * pair + side
+            center, rstd = center_ref[g], rstd_ref[g]
+            gv = par_ref[0, at(g), :] * par_ref[2, at(g), :]
+            scale = (k / count) * rstd
+            m1 = scale * jnp.sum(gv * sums_ref[1, at(g), :], axis=0, keepdims=True)
+            m2 = scale * rstd * jnp.sum(gv * sums_ref[0, at(g), :], axis=0, keepdims=True)
+            for r in tiles:
+                rows = tile(g, r)
+                slope = (0.5 * k) * rstd * (par_ref[0, rows, :] * par_ref[2, rows, :])
+                for i, c in enumerate(lanes):
+                    dev = pre_ref[rows, c] - center
+                    out[side * len(tiles) + r, i] = slope_ref[rows, c] * slope - (m1 + dev * m2)
+        for r in tiles:
+            rows = pl.ds(pl.multiple_of(2 * pair * width + 16 * r, 16), 16)
+            for i, c in enumerate(lanes):
+                both = jnp.concatenate([out[2 * r, i], out[2 * r + 1, i]])
+                pre_grad_ref[rows, c] = both.astype(BF16)
+
+    sweep(finish, GROUPS // 2, 1)
+    lane = lax.broadcasted_iota(jnp.int32, (ch, 128), 1)
+    vec = par_ref[2]
+    turned = jnp.where(lane == 0, vec * sums_ref[0], 0.0)
+    turned = jnp.where(lane == 1, vec * sums_ref[1], turned)
+    turned = jnp.where(lane == 2, sums_ref[2], turned).T[:EXTRA]
+    line = lax.broadcasted_iota(jnp.int32, turned.shape, 0)
+    k, margin = k[:, :1], margin[:, :1]
+    small_ref[...] = jnp.where(line == 3, margin * margin, turned * k)
+
+
+def head(sign, begun, turned, params, last):
+    ch, cells = begun.shape
+    return pl.pallas_call(
+        head_kernel,
+        out_shape=(jax.ShapeDtypeStruct((ch, cells), BF16), jax.ShapeDtypeStruct((EXTRA, ch), F32)),
+        in_specs=[SMEM] + [VMEM] * 7,
+        out_specs=(VMEM, VMEM),
+        scratch_shapes=[pltpu.VMEM((ch, cells), F32)] * 2
+        + [pltpu.VMEM((3, ch, 128), F32)]
+        + [pltpu.VMEM((GROUPS, 8, 128), F32)] * 2,
+        cost_estimate=pl.CostEstimate(
+            flops=3 * ch * ch * cells, bytes_accessed=8 * ch * cells, transcendentals=ch * cells
+        ),
+        compiler_params=pltpu.CompilerParams(vmem_limit_bytes=28 << 20),
+        name="head",
+    )(sign, begun, turned, params, *last)
+
+
+def add_product(begun_ref, turned_ref, refs, out_ref):
+    image = stacked(refs)
+    step = out_ref.shape[0] // 4
+    for j in range(4):
+        rows = pl.ds(j * step, step)
+        product = jnp.dot(turned_ref[rows, :], image, preferred_element_type=F32)
+        out_ref[rows, :] = product if begun_ref is None else begun_ref[rows, :] + product
+
+
+def first_kernel(turned_ref, *refs):
+    add_product(None, turned_ref, refs[:-1], refs[-1])
+
+
+def next_kernel(begun_ref, turned_ref, *refs):
+    add_product(begun_ref, turned_ref, refs[:-1], refs[-1])
+
+
+def product(begun, turned, images):
+    ch, depth = turned.shape
+    cells = images[0].shape[1]
+    args = ([] if begun is None else [begun]) + [turned, *images]
+    return pl.pallas_call(
+        first_kernel if begun is None else next_kernel,
+        out_shape=jax.ShapeDtypeStruct((ch, cells), F32),
+        in_specs=[VMEM] * len(args),
+        out_specs=VMEM,
+        input_output_aliases={} if begun is None else {0: 0},
+        cost_estimate=pl.CostEstimate(
+            flops=2 * ch * depth * cells, bytes_accessed=8 * ch * cells, transcendentals=0
+        ),
+        compiler_params=pltpu.CompilerParams(vmem_limit_bytes=14 << 20),
+        name="product",
+    )(*args)
+
+
+def image_kernel(weight_ref, pre_grad_ref, *out_refs):
+    sub = out_refs[0].shape[0]
+    grads = jnp.dot(weight_ref[...], pre_grad_ref[...], preferred_element_type=F32)
+    for i, out_ref in enumerate(out_refs):
+        out_ref[...] = grads[i * sub : (i + 1) * sub].astype(BF16)
+
+
+def grad_blocks(weight, grad_pre, parts):
+    rows, ch = weight.shape
+    cells = grad_pre.shape[1]
+    return pl.pallas_call(
+        image_kernel,
+        out_shape=(jax.ShapeDtypeStruct((rows // parts, cells), BF16),) * parts,
+        in_specs=[VMEM, VMEM],
+        out_specs=(VMEM,) * parts,
+        cost_estimate=pl.CostEstimate(
+            flops=2 * rows * ch * cells, bytes_accessed=2 * ch * cells, transcendentals=0
+        ),
+        compiler_params=pltpu.CompilerParams(vmem_limit_bytes=12 << 20),
+        name="grad_blocks",
+    )(weight, grad_pre)
+
+
+def keep_kernel(pre_grad_ref, *refs):
+    weight_columns(stacked(refs[:-1]), pre_grad_ref, refs[-1])
+
+
+def weight_keep(grad_pre, images):
+    ch, cells = grad_pre.shape
+    return pl.pallas_call(
+        keep_kernel,
+        out_shape=jax.ShapeDtypeStruct((ch // 2, ch), F32),
+        in_specs=[VMEM] * (1 + len(images)),
+        out_specs=VMEM,
+        cost_estimate=pl.CostEstimate(
+            flops=ch * ch * cells, bytes_accessed=4 * ch * cells, transcendentals=0
+        ),
+        compiler_params=pltpu.CompilerParams(vmem_limit_bytes=14 << 20),
+        name="weight_keep",
+    )(grad_pre, *images)
+
+
+def arrange_kernel(at_ref, near_ref, across_ref, core_ref, *out_refs):
+    _, sub, half = near_ref.shape
+
+    def put(row):
+        for k, masks in enumerate(SETS):
+            for i, m in enumerate(masks):
+                for side in range(2):
+                    at = (((m >> 1) & 1) * 2 + ((m >> 2) & 1)) * 2 + (m >> 3)
+                    if m & 1:
+                        block = core_ref[(side ^ row) * 8 + at]
+                    else:
+                        block = near_ref[at] if side == row else across_ref[at]
+                    out_refs[k][i * sub : (i + 1) * sub, side * half : (side + 1) * half] = block
+
+    for row in range(2):
+        pl.when(at_ref[1] == row)(functools.partial(put, row))
+
+
+def bit_order(bit):
+    return [4 * z + 2 * x + bit for z in range(4) for x in range(2)]
+
+
+def local(kernel, outs, *args, spec=None, **extra):
+    specs = [SMEM] + [VMEM] * (len(args) - 1) if spec is None else spec
+    return pl.pallas_call(
+        kernel,
+        out_shape=outs,
+        in_specs=specs,
+        cost_estimate=pl.CostEstimate(flops=1 << 21, bytes_accessed=1 << 20, transcendentals=0),
+        compiler_params=pltpu.CompilerParams(vmem_limit_bytes=14 << 20),
+        **extra,
+    )(*args)
+
+
+def rows_at(start, count):
+    return pl.ds(pl.multiple_of(start, 8), count)
+
+
+def sum1_kernel(at_ref, own_ref, pre_grad_ref, small_a, small_b, *refs):
+    images, (psend, pkeep, qsend, qkeep, total) = refs[:-5], refs[-5:]
+    weight_columns(stacked(images), pre_grad_ref, total)
+    body, cols = total.shape[0], total.shape[1] // 2
+    sub = body // 8
+    left, right = pl.ds(0, cols), pl.ds(cols, cols)
+    half, row = sub // 2, at_ref[1]
+    tail = small_a[...] + small_b[...]
+    tail = jnp.concatenate([tail[:4, :cols], tail[:4, cols:]])
+    for out, side, across in ((psend, 1 - row, 1), (pkeep, row, 0)):
+        for b in range(8):
+            rows = rows_at(b * sub + side * half, half)
+            out[b * half : (b + 1) * half, :] = own_ref[rows, left] + total[rows, left]
+        out[body // 2 :, :] = tail
+        out = qsend if out is psend else qkeep
+        for z in range(4):
+            rows = pl.ds((2 * z + across) * sub, sub)
+            out[z * sub : (z + 1) * sub, :] = own_ref[rows, right] + total[rows, right]
+
+
+def sum2_kernel(at_ref, pa, pb, qa, qb, psend, pkeep, qsend, qkeep):
+    body = pa.shape[0] - EXTRA
+    half = body // 8
+    row = at_ref[1]
+    for pout, qout, side, across in ((psend, qsend, 1 - row, 1), (pkeep, qkeep, row, 0)):
+        for z in range(4):
+            to = pl.ds(z * half, half)
+            rows = pl.ds((2 * z + across) * half, half)
+            pout[to, :] = pa[rows, :] + pb[rows, :]
+            rows = rows_at((2 * z + side) * half, half)
+            qout[to, :] = qa[rows, :] + qb[rows, :]
+        pout[body // 2 :, :] = pa[body:, :] + pb[body:, :]
+
+
+def sum3_kernel(at_ref, pa, pb, qa, qb, send, keep):
+    body, cols = qa.shape
+    half = body // 4
+    for out, side in ((send, 1), (keep, 0)):
+        for z in range(2):
+            to = pl.ds(z * half, half)
+            rows = pl.ds((2 * z + side) * half, half)
+            out[to, :cols] = pa[rows, :] + pb[rows, :]
+            out[to, cols:] = qa[rows, :] + qb[rows, :]
+        out[body // 2 :, :cols] = pa[body:, :] + pb[body:, :]
+        out[body // 2 :, cols:] = jnp.zeros((EXTRA, cols), F32)
+
+
+def sum4_kernel(at_ref, a_ref, b_ref, send, keep):
+    body = a_ref.shape[0] - EXTRA
+    for out, side in ((send, 1), (keep, 0)):
+        rows = pl.ds(side * (body // 2), body // 2)
+        out[: body // 2, :] = a_ref[rows, :] + b_ref[rows, :]
+        out[body // 2 :, :] = a_ref[body:, :] + b_ref[body:, :]
+
+
+def sum5_kernel(images, at_ref, a_ref, b_ref, part, sums, loss):
+    body, cols = part.shape[0], part.shape[1] // 2
+    part[...] = (a_ref[:body, :] + b_ref[:body, :]).astype(part.dtype)
+    tail = a_ref[body:, :cols] + b_ref[body:, :cols]
+    sums[...] = jnp.concatenate([tail[:3], tail[4:7]], axis=1)
+    loss[0] = jnp.sum(tail[3:4, :1]) / images
+
+
+def join_kernel(at_ref, part, other, out):
+    half = part.shape[0]
+    out[rows_at(at_ref[1] * half, half), :] = part[...].astype(F32)
+    out[rows_at((1 - at_ref[1]) * half, half), :] = other[...].astype(F32)
+
+
+def scatter_steps(at, sources, n, sub, ch):
+    f32 = lambda rows, cols: jax.ShapeDtypeStruct((rows, cols), F32)
+    cols, half = ch // 2, sub // 2
+    on_x = lambda v: exchange(v, "mp", n, 2)
+    on_y = lambda v: exchange(v, "dp", 2, 1)
+    outs = (f32(8 * half + EXTRA, cols),) * 2 + (f32(4 * sub, cols),) * 2
+    psend, pkeep, qsend, qkeep = local(
+        sum1_kernel, outs, at, *sources, scratch_shapes=[pltpu.VMEM((8 * sub, ch), F32)]
+    )
+    parts = pkeep, on_y(psend), qkeep, on_x(qsend)
+    outs = (f32(4 * half + EXTRA, cols),) * 2 + (f32(4 * half, cols),) * 2
+    psend, pkeep, qsend, qkeep = local(sum2_kernel, outs, at, *parts)
+    parts = pkeep, on_x(psend), qkeep, on_y(qsend)
+    send, keep = local(sum3_kernel, (f32(2 * half + EXTRA, ch),) * 2, at, *parts)
+    arrived = exchange(send, "mp", n, 4)
+    send, keep = local(sum4_kernel, (f32(half + EXTRA, ch),) * 2, at, keep, arrived)
+    arrived = exchange(send, "mp", n, 8)
+    final = jax.ShapeDtypeStruct((half, ch), BF16)
+    part, sums, loss = local(
+        functools.partial(sum5_kernel, 2 * n),
+        (final, f32(3, ch), jax.ShapeDtypeStruct((1,), F32)),
+        at,
+        keep,
+        arrived,
+        out_specs=(VMEM, VMEM, SMEM),
+    )
+    other = on_y(part)
+    return local(join_kernel, f32(sub, ch), at, part, other), sums, loss[0]
+
+
+def land_kernel(masks, at_ref, *refs):
+    count = len(masks)
+    blocks, out_ref, (wide, sems) = refs[:count], refs[-3], refs[-2:]
+    copies = []
+    for i, m in enumerate(masks):
+        wide[i] = blocks[i][...].astype(F32)
+        copies.append(pltpu.make_async_copy(wide.at[i], out_ref.at[at_ref[0] ^ m], sems.at[i]))
+        copies[-1].start()
+    for copy in copies:
+        copy.wait()
+
+
+def land(at, blocks, masks, out, n):
+    sub, cells = blocks[masks[0]].shape
+    anywhere = pl.BlockSpec(memory_space=pl.ANY)
+    args = [at] + [blocks[m] for m in masks]
+    spec = [SMEM] + [VMEM] * len(masks)
+    extra = {}
+    if out is not None:
+        args, spec = args + [out], spec + [anywhere]
+        extra["input_output_aliases"] = {len(args) - 1: 0}
+    return local(
+        functools.partial(land_kernel, masks),
+        jax.ShapeDtypeStruct((n, sub, cells), F32),
+        *args,
+        spec=spec,
+        out_specs=anywhere,
+        scratch_shapes=[
+            pltpu.VMEM((len(masks), sub, cells), F32),
+            pltpu.SemaphoreType.DMA((len(masks),)),
+        ],
+        **extra,
+    )
+
+
+def exchange(value, axis, size, mask):
+    return lax.ppermute(value, axis, [(i, i ^ mask) for i in range(size)])
+
+
+def gather_weight(block, at, n, row):
+    sub, ch = block.shape
+    half = ch // 2
+    rows = lax.dynamic_slice_in_dim(block, row * half, half, 1)[None]
+    for mask in (8, 4):
+        rows = jnp.concatenate([rows, exchange(rows, "mp", n, mask)])
+    near = jnp.concatenate([rows, exchange(rows, "mp", n, 2)])
+    across = exchange(near, "dp", 2, 1)
+    core = exchange(jnp.concatenate([near, across]), "mp", n, 1)
+    outs = tuple(jax.ShapeDtypeStruct((len(m) * sub, ch), BF16) for m in SETS)
+    return local(arrange_kernel, outs, at, near, across, core)
+
+
+def fast_shards(features, conv_weight, norm_gain, norm_bias, logit_vector, labels):
+    n, sub, _ = features.shape
+    ch = conv_weight.shape[1]
+    place, row = lax.axis_index("mp"), lax.axis_index("dp")
+    at = jnp.stack([place, row])
+    params = jnp.stack([norm_gain, norm_bias, logit_vector])
+    params = jnp.broadcast_to(params[:, :, None], (3, ch, 128))
+    image = {}
+    for m in range(n):
+        block = lax.dynamic_index_in_dim(features, place ^ m, 0, keepdims=False)
+        image[m] = exchange(block, "mp", n, m) if m else block
+    weights = gather_weight(conv_weight, at, n, row)
+    pre = None
+    for k in PRODUCTS[:-1]:
+        pre = product(pre, weights[k].T, [image[m] for m in SETS[k]])
+        pre, params = lax.optimization_barrier((pre, params))
+    twin = [exchange(image[m], "mp", n, 1) for m in bit_order(1)]
+    k = PRODUCTS[-1]
+    last = [image[m] for m in SETS[k]]
+    grad_pre, small = head(2 * labels - 1, pre, weights[k].T, params, last)
+    twin_pre = exchange(grad_pre, "mp", n, 1)
+    twin_small = exchange(small, "mp", n, 1)
+    blocks = {}
+    for k, masks in enumerate(SETS):
+        blocks.update(zip(masks, grad_blocks(weights[k], grad_pre, len(masks))))
+    landed = {}
+    for m, block in blocks.items():
+        if m in RELAYED:
+            block = exchange(block, "mp", n, m ^ 2)
+            landed[m] = exchange(block, "mp", n, 2)
+        else:
+            landed[m] = exchange(block, "mp", n, m) if m else block
+    keep = weight_keep(grad_pre, [image[m] for m in bit_order(0)])
+    sources = (keep, twin_pre, small, twin_small, *twin)
+    grad_weight, head_grads, loss = scatter_steps(at, sources, n, sub, ch)
+    grad_features = None
+    for masks in LAND:
+        grad_features = land(at, landed, masks, grad_features, n)
+    return grad_features, grad_weight, head_grads, loss
 
 
 def head_total(pre, norm_gain, norm_bias, logit_vector, signs):
@@ -53,9 +503,16 @@
     return (grad_features, grad_weight, head_grads, loss)
 
 
+SETS = ((12, 8, 13, 9), (4, 5, 1, 0), (15, 11, 6, 7), (14, 10, 2, 3))
+PRODUCTS = (0, 1, 3, 2)
+LAND = ((0, 12, 8, 13, 9), (4, 5, 1, 14, 10), (15, 11, 6, 7, 2, 3))
+RELAYED = (14, 10)
+
+
 def solution(mesh):
+    fast = mesh.shape["mp"] == 16 and mesh.shape["dp"] == 2
     return jax.shard_map(
-        shards,
+        fast_shards if fast else shards,
         mesh=mesh,
         in_specs=(P("dp", "mp", None), P("mp", None), P(), P(), P(), P(("dp", "mp"))),
         out_specs=(P("dp", "mp", None), P("mp", None), P(), P()),

time: 371 us -> 273 us (0.74)
  waiting for transfers between devices: 210 us -> 134 us
  blocking collectives: 50.3 us -> 0 us
  starting transfers between devices: 12.8 us -> 61.7 us
  Pallas kernels: 0 us -> 38.8 us
  matrix products: 31.1 us -> 0 us
  other arithmetic: 17.3 us -> 0.28 us
  between operations: 17 us -> 1.84 us
  local copies, waits for them, and re-layouts: 31.4 us -> 35.8 us
    unnamed x4 -> x0, waiting for transfers between devices: 134 us -> none
    ppermute x0 -> x54, waiting for transfers between devices: none -> 134 us  [exchange(): return lax.ppermute(value, axis, [(i, i ^ mask) for i in range(size)])]
    all_to_all x2 -> x0, waiting for transfers between devices: 76.1 us -> none  [the longest x1 76.1 us: shards(): lax.all_to_all(features, 'mp', split_axis=0, concat_axis=1, tiled=True)]
    ppermute x0 -> x54, starting transfers between devices: none -> 61.7 us  [exchange(): return lax.ppermute(value, axis, [(i, i ^ mask) for i in range(size)])]
    psum x1 -> x0, blocking collectives: 50.3 us -> none  [shards(): lax.psum((total, jnp.stack([grad_gain, grad_bias, grad_vec])), ('dp', 'mp'))]
    pallas_call x0 -> x19, Pallas kernels: none -> 38.8 us  [the longest x10 14.2 us: local(): pl.pallas_call(kernel, out_shape=outs, in_specs=specs, cost_estimate=pl.C...]
    dot_general x3 -> x0, matrix products: 31.1 us -> none  [the longest x1 12.1 us: shards(): jnp.einsum('io,nos->nis', weight_full, grad_pre, preferred_element_type=j...]
    reduce_sum x9 -> x0, other arithmetic: 16.6 us -> none  [the longest x4 6.37 us: head_total(): spread = jnp.mean((grouped - center) ** 2, axis=(2, 3), keepdims=True)]
  transfers between devices with their start and end apart: 5 -> 54, of which waited for: 2 -> 23; matrix products, arithmetic and copies ran while one was open for 9% -> 4% of each run, Pallas kernels for 0% -> 9%
where the time goes in v1:
time: 273 us; the launch traced here: 272 us
  waiting for transfers between devices  134 us (49%)
  starting transfers between devices  61.7 us (23%)
  Pallas kernels  38.8 us (14%)
  local copies, waits for them, and re-layouts  35.8 us (13%)
    ppermute x54, waiting for transfers between devices, exchange(): return lax.ppermute(value, axis, [(i, i ^ mask) for i in range(size)])  134 us
    ppermute x54, starting transfers between devices, exchange(): return lax.ppermute(value, axis, [(i, i ^ mask) for i in range(size)])  61.7 us
    unnamed x68, local copies, waits for them, and re-layouts  25.6 us
    pallas_call x10, Pallas kernels, local(): pl.pallas_call(kernel, out_shape=outs, in_specs=specs, cost_estimate=pl.C...  14.2 us
    pallas_call x1, Pallas kernels, head(): pl.pallas_call(head_kernel, out_shape=(jax.ShapeDtypeStruct((ch, cells),...  10.1 us
    pallas_call x3, Pallas kernels, product(): pl.pallas_call(first_kernel if begun is None else next_kernel, out_shape=...  7.36 us
  transfers between devices with their start and end apart: 54, of which 23 were waited for; matrix products, arithmetic and copies ran while one was open for 4% of the time, Pallas kernels for 9%

profile of v1, /device:TPU:12, one launch (start us, length us, event | category | flops | bytes accessed | tf_op | source)
XLA Modules:
  0.0 272.2 jit_solution(16972754321102243854)
XLA Ops:
  2.2 2.6 collective-permute-start
  4.8 4.2 %collective-permute-done = bf16[1,80,640]{2,1,0:T(8,128)(2,1)S(1)} collective-permute-done((bf16[1,80,640]{2,1,0:T(8,128)(2,1)S(1)}, bf16[1,80,640]{2,1,0:T(8,128)(2,1)S(1)}, u32[]{:S(2)}, u32[]{:S(2)}) %collective-permute-start) | collective-permute-done | bytes 102432 | tf_op jit(solution)/shard_map/ppermute | solution.py:405
  10.5 5.6 %collective-permute-done.1 = bf16[2,80,640]{2,1,0:T(8,128)(2,1)S(1)} collective-permute-done((bf16[2,80,640]{2,1,0:T(8,128)(2,1)S(1)}, bf16[2,80,640]{2,1,0:T(8,128)(2,1)S(1)}, u32[]{:S(2)}, u32[]{:S(2)}) %collective-permute-start.1) | collective-permute-done | bytes 204832 | tf_op jit(solution)/shard_map/ppermute | solution.py:405
  17.7 9.0 %collective-permute-done.2 = bf16[4,80,640]{2,1,0:T(8,128)(2,1)S(1)} collective-permute-done((bf16[4,80,640]{2,1,0:T(8,128)(2,1)S(1)}, bf16[4,80,640]{2,1,0:T(8,128)(2,1)S(1)}, u32[]{:S(2)}, u32[]{:S(2)}) %collective-permute-start.2) | collective-permute-done | bytes 409632 | tf_op jit(solution)/shard_map/ppermute | solution.py:405
  29.6 15.8 %collective-permute-done.3.across_ref = bf16[8,80,640]{2,1,0:T(8,128)(2,1)S(1)} collective-permute-done((bf16[8,80,640]{2,1,0:T(8,128)(2,1)S(1)}, bf16[8,80,640]{2,1,0:T(8,128)(2,1)S(1)}, u32[]{:S(2)}, u32[]{:S(2)}) %collective-permute-start.3) | collective-permute-done | bytes 819232 | tf_op jit(solution)/shard_map/ppermute | solution.py:405
  46.4 3.0 %dynamic-slice_bitcast_fusion = (bf16[80,1024]{1,0:T(8,128)(2,1)}, bf16[80,1024]{1,0:T(8,128)(2,1)}, bf16[80,1024]{1,0:T(8,128)(2,1)}, bf16[80,1024]{1,0:T(8,128...) fusion(bf16[16,80,1024]{2,1,0:T(8,128)(2,1)} %param.6, ...), kind=kLoop, calls=%fused_computation.3 | loop fusion | bytes 5242944 | tf_op jit(solution)/shard_map/jit(dynamic_index_in_dim)/squeeze | solution.py:430
  49.3 2.8 %collective-permute-start.5 = (bf16[80,1024]{1,0:T(8,128)(2,1)S(1)}, bf16[80,1024]{1,0:T(8,128)(2,1)S(1)}, u32[]{:S(2)}, u32[]{:S(2)}) collective-permute-start(bf16[80,1024]{1,0:T(8,128)(2,1)S(1)} %get-tuple-element.106), channel_id=1, source_target_pairs={{0,12},{1,13},{2,14},{3,15},{4,8},{5,9},{6,10},{7,11},{8,4},{9,5},... | collective-permute-start | bytes 491528 | tf_op jit(solution)/shard_map/ppermute | solution.py:405
  56.3 14.9 %collective-permute-done.5.refs_0_.refs_6_ = bf16[80,1024]{1,0:T(8,128)(2,1)S(1)} collective-permute-done((bf16[80,1024]{1,0:T(8,128)(2,1)S(1)}, bf16[80,1024]{1,0:T(8,128)(2,1)S(1)}, u32[]{:S(2)}, u32[]{:S(2)}) %collective-permute-start.5) | collective-permute-done | bytes 163872 | tf_op jit(solution)/shard_map/ppermute | solution.py:405
  75.0 2.8 %collective-permute-done.7.refs_2_ = bf16[80,1024]{1,0:T(8,128)(2,1)S(1)} collective-permute-done((bf16[80,1024]{1,0:T(8,128)(2,1)S(1)}, bf16[80,1024]{1,0:T(8,128)(2,1)S(1)}, u32[]{:S(2)}, u32[]{:S(2)}) %collective-permute-start.7) | collective-permute-done | bytes 163872 | tf_op jit(solution)/shard_map/ppermute | solution.py:405
  83.3 4.1 %collective-permute-start.13 = (bf16[80,1024]{1,0:T(8,128)(2,1)}, bf16[80,1024]{1,0:T(8,128)(2,1)}, u32[]{:S(2)}, u32[]{:S(2)}) collective-permute-start(bf16[80,1024]{1,0:T(8,128)(2,1)} %get-tuple-element.97), channel_id=1, source_target_pairs={{0,10},{1,11},{2,8},{3,9},{4,14},{5,15},{6,12},{7,13},{8,2},{9,3},... | collective-permute-start | bytes 491528 | tf_op jit(solution)/shard_map/ppermute | solution.py:405
  95.6 2.7 collective-permute-start.16
  98.6 2.8 %collective-permute-start.18 = (bf16[80,1024]{1,0:T(8,128)(2,1)}, bf16[80,1024]{1,0:T(8,128)(2,1)}, u32[]{:S(2)}, u32[]{:S(2)}) collective-permute-start(bf16[80,1024]{1,0:T(8,128)(2,1)} %get-tuple-element.107), channel_id=1, source_target_pairs={{0,6},{1,7},{2,4},{3,5},{4,2},{5,3},{6,0},{7,1},{8,14},{9,15},{10,... | collective-permute-start | bytes 491528 | tf_op jit(solution)/shard_map/ppermute | solution.py:405
  108.9 2.5 copy-done.1
  111.4 2.8 %product.4.begun_ref = f32[1280,1024]{1,0:T(8,128)S(1)} custom-call(f32[1280,1024]{1,0:T(8,128)S(1)} %copy-done.1, bf16[1280,320]{1,0:T(8,128)(2,1)S(1)} %bitcast.44, bf16[80,1024]{1,0:T(8,128)(2,1)} %collective-permute-done.9.refs_0_.refs_2_, bf16[80,1024]{1,0:T(8,128)(2,1)S(1)} %copy-done.24, ...), custom_call_target="tpu_custom_call", output_to_operand_aliasing={{}: (0, {})} | custom-call | flops 838860800 | bytes 10485760 | tf_op jit(solution)/shard_map/product/pallas_call | solution.py:176
  119.7 3.0 %product.5.begun_ref = f32[1280,1024]{1,0:T(8,128)S(1)} custom-call(f32[1280,1024]{1,0:T(8,128)S(1)} %copy-done.3, bf16[1280,320]{1,0:T(8,128)(2,1)S(1)} %bitcast.43, bf16[80,1024]{1,0:T(8,128)(2,1)} %collective-permute-done.12.refs_0_.refs_7_, bf16[80,1024]{1,0:T(8,128)(2,1)} %collective-permute-done.13.refs_1_.refs_5_, ...), custom_call_target="tpu_custom_call", output_to_operand_aliasing={{}: (0, {})} | custom-call | flops 838860800 | bytes 10485760 | tf_op jit(solution)/shard_map/product/pallas_call | solution.py:176
  125.8 2.5 copy-done.5
  129.8 10.1 %head.1 = (bf16[1280,1024]{1,0:T(8,128)(2,1)S(1)}, f32[8,1280]{1,0:T(8,128)S(1)}) custom-call(s32[1]{0:T(128)S(6)} %sub.3.info_ref, f32[1280,1024]{1,0:T(8,128)S(1)} %copy-done.5, bf16[1280,320]{1,0:T(8,128)(2,1)S(1)} %bitcast.45, f32[3,1280,128]{2,1,0:T(8,128)S(1)} %copy-done.10, bf16[80,1024]{1,0:T(8,128)(2,1)} %collective-permute-done.16.refs_0_, ...), custom_call_target="tpu_custom_call" | custom-call | flops 5033164800 | bytes 10485760 | tf_op jit(solution)/shard_map/head/pallas_call | solution.py:139
  141.1 4.0 %collective-permute-done.39.refs_0_ = bf16[80,1024]{1,0:T(8,128)(2,1)S(1)} collective-permute-done((bf16[80,1024]{1,0:T(8,128)(2,1)S(1)}, bf16[80,1024]{1,0:T(8,128)(2,1)S(1)}, u32[]{:S(2)}, u32[]{:S(2)}) %collective-permute-start.39) | collective-permute-done | bytes 163872 | tf_op jit(solution)/shard_map/ppermute | solution.py:405
  146.7 3.1 %weight_keep.1.own_ref = f32[640,1280]{1,0:T(8,128)S(1)} custom-call(bf16[1280,1024]{1,0:T(8,128)(2,1)S(1)} %get-tuple-element.57.pre_grad_ref, bf16[80,1024]{1,0:T(8,128)(2,1)S(1)} %get-tuple-element.99.refs_3_.refs_0_, bf16[80,1024]{1,0:T(8,128)(2,1)} %collective-permute-done.14.refs_2_.refs_1_, bf16[80,1024]{1,0:T(8,128)(2,1)} %collective-permute-done.9.refs_0_.refs_2_, ...), custom_call_target="tpu_custom_call" | custom-call | flops 1677721600 | bytes 5242880 | tf_op jit(solution)/shard_map/weight_keep/pallas_call | solution.py:219
  149.9 2.6 shard_map.97
  153.6 19.7 %collective-permute-done.48.qb = f32[320,640]{1,0:T(8,128)S(1)} collective-permute-done((f32[320,640]{1,0:T(8,128)S(1)}, f32[320,640]{1,0:T(8,128)S(1)}, u32[]{:S(2)}, u32[]{:S(2)}) %collective-permute-start.48) | collective-permute-done | bytes 819232 | tf_op jit(solution)/shard_map/ppermute | solution.py:405
  176.2 9.3 %collective-permute-done.50.qb = f32[160,640]{1,0:T(8,128)S(1)} collective-permute-done((f32[160,640]{1,0:T(8,128)S(1)}, f32[160,640]{1,0:T(8,128)S(1)}, u32[]{:S(2)}, u32[]{:S(2)}) %collective-permute-start.50) | collective-permute-done | bytes 409632 | tf_op jit(solution)/shard_map/ppermute | solution.py:405
  189.6 7.8 %collective-permute-start.33 = (bf16[80,1024]{1,0:T(8,128)(2,1)S(1)}, bf16[80,1024]{1,0:T(8,128)(2,1)S(1)}, u32[]{:S(2)}, u32[]{:S(2)}) collective-permute-start(bf16[80,1024]{1,0:T(8,128)(2,1)S(1)} %get-tuple-element.70), channel_id=1, source_target_pairs={{0,12},{1,13},{2,14},{3,15},{4,8},{5,9},{6,10},{7,11},{8,4},{9,5},... | collective-permute-start | bytes 491528 | tf_op jit(solution)/shard_map/ppermute | solution.py:405
  197.4 3.6 %collective-permute-start.36 = (bf16[80,1024]{1,0:T(8,128)(2,1)S(1)}, bf16[80,1024]{1,0:T(8,128)(2,1)S(1)}, u32[]{:S(2)}, u32[]{:S(2)}) collective-permute-start(bf16[80,1024]{1,0:T(8,128)(2,1)S(1)} %get-tuple-element.73), channel_id=1, source_target_pairs={{0,9},{1,8},{2,11},{3,10},{4,13},{5,12},{6,15},{7,14},{8,1},{9,0},... | collective-permute-start | bytes 491528 | tf_op jit(solution)/shard_map/ppermute | solution.py:405
  202.0 11.9 %collective-permute-done.33.refs_1_ = bf16[80,1024]{1,0:T(8,128)(2,1)S(1)} collective-permute-done((bf16[80,1024]{1,0:T(8,128)(2,1)S(1)}, bf16[80,1024]{1,0:T(8,128)(2,1)S(1)}, u32[]{:S(2)}, u32[]{:S(2)}) %collective-permute-start.33) | collective-permute-done | bytes 163872 | tf_op jit(solution)/shard_map/ppermute | solution.py:405
  213.9 3.6 %collective-permute-done.34.refs_2_ = bf16[80,1024]{1,0:T(8,128)(2,1)S(1)} collective-permute-done((bf16[80,1024]{1,0:T(8,128)(2,1)S(1)}, bf16[80,1024]{1,0:T(8,128)(2,1)S(1)}, u32[]{:S(2)}, u32[]{:S(2)}) %collective-permute-start.34) | collective-permute-done | bytes 163872 | tf_op jit(solution)/shard_map/ppermute | solution.py:405
  217.5 3.5 %collective-permute-done.35.refs_3_ = bf16[80,1024]{1,0:T(8,128)(2,1)S(1)} collective-permute-done((bf16[80,1024]{1,0:T(8,128)(2,1)S(1)}, bf16[80,1024]{1,0:T(8,128)(2,1)S(1)}, u32[]{:S(2)}, u32[]{:S(2)}) %collective-permute-start.35) | collective-permute-done | bytes 163872 | tf_op jit(solution)/shard_map/ppermute | solution.py:405
  229.8 13.2 %collective-permute-done.29 = bf16[80,1024]{1,0:T(8,128)(2,1)S(1)} collective-permute-done((bf16[80,1024]{1,0:T(8,128)(2,1)S(1)}, bf16[80,1024]{1,0:T(8,128)(2,1)S(1)}, u32[]{:S(2)}, u32[]{:S(2)}) %collective-permute-start.29) | collective-permute-done | bytes 163872 | tf_op jit(solution)/shard_map/ppermute | solution.py:405
  246.7 6.5 %collective-permute-start.21 = (bf16[80,1024]{1,0:T(8,128)(2,1)S(1)}, bf16[80,1024]{1,0:T(8,128)(2,1)S(1)}, u32[]{:S(2)}, u32[]{:S(2)}) collective-permute-start(bf16[80,1024]{1,0:T(8,128)(2,1)S(1)} %get-tuple-element.59), channel_id=1, source_target_pairs={{0,11},{1,10},{2,9},{3,8},{4,15},{5,14},{6,13},{7,12},{8,3},{9,2},... | collective-permute-start | bytes 491528 | tf_op jit(solution)/shard_map/ppermute | solution.py:405
  258.8 4.1 %collective-permute-done.20.refs_0_ = bf16[80,1024]{1,0:T(8,128)(2,1)S(1)} collective-permute-done((bf16[80,1024]{1,0:T(8,128)(2,1)S(1)}, bf16[80,1024]{1,0:T(8,128)(2,1)S(1)}, u32[]{:S(2)}, u32[]{:S(2)}) %collective-permute-start.20) | collective-permute-done | bytes 163872 | tf_op jit(solution)/shard_map/ppermute | solution.py:405
  262.9 2.8 %collective-permute-done.21.refs_1_ = bf16[80,1024]{1,0:T(8,128)(2,1)S(1)} collective-permute-done((bf16[80,1024]{1,0:T(8,128)(2,1)S(1)}, bf16[80,1024]{1,0:T(8,128)(2,1)S(1)}, u32[]{:S(2)}, u32[]{:S(2)}) %collective-permute-start.21) | collective-permute-done | bytes 163872 | tf_op jit(solution)/shard_map/ppermute | solution.py:405
  265.7 3.3 %collective-permute-done.23.refs_3_ = bf16[80,1024]{1,0:T(8,128)(2,1)S(1)} collective-permute-done((bf16[80,1024]{1,0:T(8,128)(2,1)S(1)}, bf16[80,1024]{1,0:T(8,128)(2,1)S(1)}, u32[]{:S(2)}, u32[]{:S(2)}) %collective-permute-start.23) | collective-permute-done | bytes 163872 | tf_op jit(solution)/shard_map/ppermute | solution.py:405
  (178 shorter events, 80.0 us)
Async XLA Ops:
  26.9 18.5 %collective-permute-start.3 = (bf16[8,80,640]{2,1,0:T(8,128)(2,1)S(1)}, bf16[8,80,640]{2,1,0:T(8,128)(2,1)S(1)}, u32[]{:S(2)}, u32[]{:S(2)}) collective-permute-start(bf16[8,80,640]{2,1,0:T(8,128)(2,1)S(1)} %pad_maximum_fusion.near_ref), channel_id=1, source_target_pairs={{0,16},{16,0},{1,17},{17,1},{2,18},{18,2},{3,19},{19,3},{4,20},{20... | collective-permute-start | bytes 2457608 | tf_op jit(solution)/shard_map/ppermute | solution.py:405
  46.3 43.3 %collective-permute-start.4 = (bf16[16,80,640]{2,1,0:T(8,128)(2,1)}, bf16[16,80,640]{2,1,0:T(8,128)(2,1)}, u32[]{:S(2)}, u32[]{:S(2)}) collective-permute-start(bf16[16,80,640]{2,1,0:T(8,128)(2,1)} %constant_dynamic-update-slice_fusion), channel_id=1, source_target_pairs={{0,1},{1,0},{2,3},{3,2},{4,5},{5,4},{6,7},{7,6},{8,9},{9,8},{10,11... | collective-permute-start | bytes 4915208 | tf_op jit(solution)/shard_map/ppermute | solution.py:405
  49.3 21.9 %collective-permute-start.5 = (bf16[80,1024]{1,0:T(8,128)(2,1)S(1)}, bf16[80,1024]{1,0:T(8,128)(2,1)S(1)}, u32[]{:S(2)}, u32[]{:S(2)}) collective-permute-start(bf16[80,1024]{1,0:T(8,128)(2,1)S(1)} %get-tuple-element.106), channel_id=1, source_target_pairs={{0,12},{1,13},{2,14},{3,15},{4,8},{5,9},{6,10},{7,11},{8,4},{9,5},... | collective-permute-start | bytes 491528 | tf_op jit(solution)/shard_map/ppermute | solution.py:405
  52.1 22.1 %collective-permute-start.6 = (bf16[80,1024]{1,0:T(8,128)(2,1)S(1)}, bf16[80,1024]{1,0:T(8,128)(2,1)S(1)}, u32[]{:S(2)}, u32[]{:S(2)}) collective-permute-start(bf16[80,1024]{1,0:T(8,128)(2,1)S(1)} %get-tuple-element.105), channel_id=1, source_target_pairs={{0,8},{1,9},{2,10},{3,11},{4,12},{5,13},{6,14},{7,15},{8,0},{9,1},... | collective-permute-start | bytes 491528 | tf_op jit(solution)/shard_map/ppermute | solution.py:405
  52.8 25.0 %collective-permute-start.7 = (bf16[80,1024]{1,0:T(8,128)(2,1)S(1)}, bf16[80,1024]{1,0:T(8,128)(2,1)S(1)}, u32[]{:S(2)}, u32[]{:S(2)}) collective-permute-start(bf16[80,1024]{1,0:T(8,128)(2,1)S(1)} %get-tuple-element.104), channel_id=1, source_target_pairs={{0,13},{1,12},{2,15},{3,14},{4,9},{5,8},{6,11},{7,10},{8,5},{9,4},... | collective-permute-start | bytes 491528 | tf_op jit(solution)/shard_map/ppermute | solution.py:405
  55.2 25.6 %collective-permute-start.8 = (bf16[80,1024]{1,0:T(8,128)(2,1)S(1)}, bf16[80,1024]{1,0:T(8,128)(2,1)S(1)}, u32[]{:S(2)}, u32[]{:S(2)}) collective-permute-start(bf16[80,1024]{1,0:T(8,128)(2,1)S(1)} %get-tuple-element.103), channel_id=1, source_target_pairs={{0,9},{1,8},{2,11},{3,10},{4,13},{5,12},{6,15},{7,14},{8,1},{9,0},... | collective-permute-start | bytes 491528 | tf_op jit(solution)/shard_map/ppermute | solution.py:405
  78.5 17.1 %collective-permute-start.9 = (bf16[80,1024]{1,0:T(8,128)(2,1)}, bf16[80,1024]{1,0:T(8,128)(2,1)}, u32[]{:S(2)}, u32[]{:S(2)}) collective-permute-start(bf16[80,1024]{1,0:T(8,128)(2,1)} %get-tuple-element.102), channel_id=1, source_target_pairs={{0,4},{1,5},{2,6},{3,7},{4,0},{5,1},{6,2},{7,3},{8,12},{9,13},{10,... | collective-permute-start | bytes 491528 | tf_op jit(solution)/shard_map/ppermute | solution.py:405
  81.5 16.8 %collective-permute-start.12 = (bf16[80,1024]{1,0:T(8,128)(2,1)}, bf16[80,1024]{1,0:T(8,128)(2,1)}, u32[]{:S(2)}, u32[]{:S(2)}) collective-permute-start(bf16[80,1024]{1,0:T(8,128)(2,1)} %get-tuple-element.98), channel_id=1, source_target_pairs={{0,14},{1,15},{2,12},{3,13},{4,10},{5,11},{6,8},{7,9},{8,6},{9,7},... | collective-permute-start | bytes 491528 | tf_op jit(solution)/shard_map/ppermute | solution.py:405
  83.3 15.3 %collective-permute-start.13 = (bf16[80,1024]{1,0:T(8,128)(2,1)}, bf16[80,1024]{1,0:T(8,128)(2,1)}, u32[]{:S(2)}, u32[]{:S(2)}) collective-permute-start(bf16[80,1024]{1,0:T(8,128)(2,1)} %get-tuple-element.97), channel_id=1, source_target_pairs={{0,10},{1,11},{2,8},{3,9},{4,14},{5,15},{6,12},{7,13},{8,2},{9,3},... | collective-permute-start | bytes 491528 | tf_op jit(solution)/shard_map/ppermute | solution.py:405
  88.1 13.3 %collective-permute-start.14 = (bf16[80,1024]{1,0:T(8,128)(2,1)}, bf16[80,1024]{1,0:T(8,128)(2,1)}, u32[]{:S(2)}, u32[]{:S(2)}) collective-permute-start(bf16[80,1024]{1,0:T(8,128)(2,1)} %get-tuple-element.96), channel_id=1, source_target_pairs={{0,2},{1,3},{2,0},{3,1},{4,6},{5,7},{6,4},{7,5},{8,10},{9,11},{10,... | collective-permute-start | bytes 491528 | tf_op jit(solution)/shard_map/ppermute | solution.py:405
  89.6 27.6 %collective-permute-start.15 = (bf16[80,1024]{1,0:T(8,128)(2,1)}, bf16[80,1024]{1,0:T(8,128)(2,1)}, u32[]{:S(2)}, u32[]{:S(2)}) collective-permute-start(bf16[80,1024]{1,0:T(8,128)(2,1)} %get-tuple-element.95), channel_id=1, source_target_pairs={{0,3},{1,2},{2,1},{3,0},{4,7},{5,6},{6,5},{7,4},{8,11},{9,10},{10,... | collective-permute-start | bytes 491528 | tf_op jit(solution)/shard_map/ppermute | solution.py:405
  95.6 30.1 %collective-permute-start.16 = (bf16[80,1024]{1,0:T(8,128)(2,1)}, bf16[80,1024]{1,0:T(8,128)(2,1)}, u32[]{:S(2)}, u32[]{:S(2)}) collective-permute-start(bf16[80,1024]{1,0:T(8,128)(2,1)} %get-tuple-element.94), channel_id=1, source_target_pairs={{0,15},{1,14},{2,13},{3,12},{4,11},{5,10},{6,9},{7,8},{8,7},{9,6},... | collective-permute-start | bytes 491528 | tf_op jit(solution)/shard_map/ppermute | solution.py:405
  98.3 27.4 %collective-permute-start.17 = (bf16[80,1024]{1,0:T(8,128)(2,1)}, bf16[80,1024]{1,0:T(8,128)(2,1)}, u32[]{:S(2)}, u32[]{:S(2)}) collective-permute-start(bf16[80,1024]{1,0:T(8,128)(2,1)} %get-tuple-element.93), channel_id=1, source_target_pairs={{0,11},{1,10},{2,9},{3,8},{4,15},{5,14},{6,13},{7,12},{8,3},{9,2},... | collective-permute-start | bytes 491528 | tf_op jit(solution)/shard_map/ppermute | solution.py:405
  98.6 27.1 %collective-permute-start.18 = (bf16[80,1024]{1,0:T(8,128)(2,1)}, bf16[80,1024]{1,0:T(8,128)(2,1)}, u32[]{:S(2)}, u32[]{:S(2)}) collective-permute-start(bf16[80,1024]{1,0:T(8,128)(2,1)} %get-tuple-element.107), channel_id=1, source_target_pairs={{0,6},{1,7},{2,4},{3,5},{4,2},{5,3},{6,0},{7,1},{8,14},{9,15},{10,... | collective-permute-start | bytes 491528 | tf_op jit(solution)/shard_map/ppermute | solution.py:405
  101.5 24.3 %collective-permute-start.19 = (bf16[80,1024]{1,0:T(8,128)(2,1)}, bf16[80,1024]{1,0:T(8,128)(2,1)}, u32[]{:S(2)}, u32[]{:S(2)}) collective-permute-start(bf16[80,1024]{1,0:T(8,128)(2,1)} %get-tuple-element.92), channel_id=1, source_target_pairs={{0,7},{1,6},{2,5},{3,4},{4,3},{5,2},{6,1},{7,0},{8,15},{9,14},{10,... | collective-permute-start | bytes 491528 | tf_op jit(solution)/shard_map/ppermute | solution.py:405
  152.5 21.0 %collective-permute-start.47 = (f32[328,640]{1,0:T(8,128)S(1)}, f32[328,640]{1,0:T(8,128)S(1)}, u32[]{:S(2)}, u32[]{:S(2)}) collective-permute-start(f32[328,640]{1,0:T(8,128)S(1)} %get-tuple-element.76), channel_id=1, source_target_pairs={{0,16},{16,0},{1,17},{17,1},{2,18},{18,2},{3,19},{19,3},{4,20},{20... | collective-permute-start | bytes 2519048 | tf_op jit(solution)/shard_map/ppermute | solution.py:405
  153.1 20.2 %collective-permute-start.48 = (f32[320,640]{1,0:T(8,128)S(1)}, f32[320,640]{1,0:T(8,128)S(1)}, u32[]{:S(2)}, u32[]{:S(2)}) collective-permute-start(f32[320,640]{1,0:T(8,128)S(1)} %get-tuple-element.78), channel_id=1, source_target_pairs={{0,2},{1,3},{2,0},{3,1},{4,6},{5,7},{6,4},{7,5},{8,10},{9,11},{10,... | collective-permute-start | bytes 2457608 | tf_op jit(solution)/shard_map/ppermute | solution.py:405
  186.3 38.4 %collective-permute-start.51 = (f32[88,1280]{1,0:T(8,128)S(1)}, f32[88,1280]{1,0:T(8,128)S(1)}, u32[]{:S(2)}, u32[]{:S(2)}) collective-permute-start(f32[88,1280]{1,0:T(8,128)S(1)} %get-tuple-element.84), channel_id=1, source_target_pairs={{0,4},{1,5},{2,6},{3,7},{4,0},{5,1},{6,2},{7,3},{8,12},{9,13},{10,... | collective-permute-start | bytes 1351688 | tf_op jit(solution)/shard_map/ppermute | solution.py:405
  189.6 24.3 %collective-permute-start.33 = (bf16[80,1024]{1,0:T(8,128)(2,1)S(1)}, bf16[80,1024]{1,0:T(8,128)(2,1)S(1)}, u32[]{:S(2)}, u32[]{:S(2)}) collective-permute-start(bf16[80,1024]{1,0:T(8,128)(2,1)S(1)} %get-tuple-element.70), channel_id=1, source_target_pairs={{0,12},{1,13},{2,14},{3,15},{4,8},{5,9},{6,10},{7,11},{8,4},{9,5},... | collective-permute-start | bytes 491528 | tf_op jit(solution)/shard_map/ppermute | solution.py:405
  197.3 20.1 %collective-permute-start.34 = (bf16[80,1024]{1,0:T(8,128)(2,1)S(1)}, bf16[80,1024]{1,0:T(8,128)(2,1)S(1)}, u32[]{:S(2)}, u32[]{:S(2)}) collective-permute-start(bf16[80,1024]{1,0:T(8,128)(2,1)S(1)} %get-tuple-element.71), channel_id=1, source_target_pairs={{0,8},{1,9},{2,10},{3,11},{4,12},{5,13},{6,14},{7,15},{8,0},{9,1},... | collective-permute-start | bytes 491528 | tf_op jit(solution)/shard_map/ppermute | solution.py:405
  197.4 23.6 %collective-permute-start.35 = (bf16[80,1024]{1,0:T(8,128)(2,1)S(1)}, bf16[80,1024]{1,0:T(8,128)(2,1)S(1)}, u32[]{:S(2)}, u32[]{:S(2)}) collective-permute-start(bf16[80,1024]{1,0:T(8,128)(2,1)S(1)} %get-tuple-element.72), channel_id=1, source_target_pairs={{0,13},{1,12},{2,15},{3,14},{4,9},{5,8},{6,11},{7,10},{8,5},{9,4},... | collective-permute-start | bytes 491528 | tf_op jit(solution)/shard_map/ppermute | solution.py:405
  197.4 26.2 %collective-permute-start.36 = (bf16[80,1024]{1,0:T(8,128)(2,1)S(1)}, bf16[80,1024]{1,0:T(8,128)(2,1)S(1)}, u32[]{:S(2)}, u32[]{:S(2)}) collective-permute-start(bf16[80,1024]{1,0:T(8,128)(2,1)S(1)} %get-tuple-element.73), channel_id=1, source_target_pairs={{0,9},{1,8},{2,11},{3,10},{4,13},{5,12},{6,15},{7,14},{8,1},{9,0},... | collective-permute-start | bytes 491528 | tf_op jit(solution)/shard_map/ppermute | solution.py:405
  213.9 12.6 %collective-permute-start.26 = (bf16[80,1024]{1,0:T(8,128)(2,1)S(1)}, bf16[80,1024]{1,0:T(8,128)(2,1)S(1)}, u32[]{:S(2)}, u32[]{:S(2)}) collective-permute-start(bf16[80,1024]{1,0:T(8,128)(2,1)S(1)} %get-tuple-element.64), channel_id=1, source_target_pairs={{0,4},{1,5},{2,6},{3,7},{4,0},{5,1},{6,2},{7,3},{8,12},{9,13},{10,... | collective-permute-start | bytes 491528 | tf_op jit(solution)/shard_map/ppermute | solution.py:405
  223.6 19.4 %collective-permute-start.29 = (bf16[80,1024]{1,0:T(8,128)(2,1)S(1)}, bf16[80,1024]{1,0:T(8,128)(2,1)S(1)}, u32[]{:S(2)}, u32[]{:S(2)}) collective-permute-start(bf16[80,1024]{1,0:T(8,128)(2,1)S(1)} %get-tuple-element.67), channel_id=1, source_target_pairs={{0,12},{1,13},{2,14},{3,15},{4,8},{5,9},{6,10},{7,11},{8,4},{9,5},... | collective-permute-start | bytes 491528 | tf_op jit(solution)/shard_map/ppermute | solution.py:405
  224.7 19.8 %collective-permute-start.31 = (bf16[80,1024]{1,0:T(8,128)(2,1)S(1)}, bf16[80,1024]{1,0:T(8,128)(2,1)S(1)}, u32[]{:S(2)}, u32[]{:S(2)}) collective-permute-start(bf16[80,1024]{1,0:T(8,128)(2,1)S(1)} %get-tuple-element.68), channel_id=1, source_target_pairs={{0,8},{1,9},{2,10},{3,11},{4,12},{5,13},{6,14},{7,15},{8,0},{9,1},... | collective-permute-start | bytes 491528 | tf_op jit(solution)/shard_map/ppermute | solution.py:405
  226.5 26.7 %collective-permute-start.52 = (f32[48,1280]{1,0:T(8,128)S(1)}, f32[48,1280]{1,0:T(8,128)S(1)}, u32[]{:S(2)}, u32[]{:S(2)}) collective-permute-start(f32[48,1280]{1,0:T(8,128)S(1)} %get-tuple-element.86), channel_id=1, source_target_pairs={{0,8},{1,9},{2,10},{3,11},{4,12},{5,13},{6,14},{7,15},{8,0},{9,1},... | collective-permute-start | bytes 737288 | tf_op jit(solution)/shard_map/ppermute | solution.py:405
  228.3 18.3 %collective-permute-start.24 = (bf16[80,1024]{1,0:T(8,128)(2,1)S(1)}, bf16[80,1024]{1,0:T(8,128)(2,1)S(1)}, u32[]{:S(2)}, u32[]{:S(2)}) collective-permute-start(bf16[80,1024]{1,0:T(8,128)(2,1)S(1)} %get-tuple-element.62), channel_id=1, source_target_pairs={{0,2},{1,3},{2,0},{3,1},{4,6},{5,7},{6,4},{7,5},{8,10},{9,11},{10,... | collective-permute-start | bytes 491528 | tf_op jit(solution)/shard_map/ppermute | solution.py:405
  229.3 17.4 %collective-permute-start.25 = (bf16[80,1024]{1,0:T(8,128)(2,1)S(1)}, bf16[80,1024]{1,0:T(8,128)(2,1)S(1)}, u32[]{:S(2)}, u32[]{:S(2)}) collective-permute-start(bf16[80,1024]{1,0:T(8,128)(2,1)S(1)} %get-tuple-element.63), channel_id=1, source_target_pairs={{0,3},{1,2},{2,1},{3,0},{4,7},{5,6},{6,5},{7,4},{8,11},{9,10},{10,... | collective-permute-start | bytes 491528 | tf_op jit(solution)/shard_map/ppermute | solution.py:405
  246.6 16.3 %collective-permute-start.20 = (bf16[80,1024]{1,0:T(8,128)(2,1)S(1)}, bf16[80,1024]{1,0:T(8,128)(2,1)S(1)}, u32[]{:S(2)}, u32[]{:S(2)}) collective-permute-start(bf16[80,1024]{1,0:T(8,128)(2,1)S(1)} %get-tuple-element.58), channel_id=1, source_target_pairs={{0,15},{1,14},{2,13},{3,12},{4,11},{5,10},{6,9},{7,8},{8,7},{9,6},... | collective-permute-start | bytes 491528 | tf_op jit(solution)/shard_map/ppermute | solution.py:405
  246.7 19.0 %collective-permute-start.21 = (bf16[80,1024]{1,0:T(8,128)(2,1)S(1)}, bf16[80,1024]{1,0:T(8,128)(2,1)S(1)}, u32[]{:S(2)}, u32[]{:S(2)}) collective-permute-start(bf16[80,1024]{1,0:T(8,128)(2,1)S(1)} %get-tuple-element.59), channel_id=1, source_target_pairs={{0,11},{1,10},{2,9},{3,8},{4,15},{5,14},{6,13},{7,12},{8,3},{9,2},... | collective-permute-start | bytes 491528 | tf_op jit(solution)/shard_map/ppermute | solution.py:405
  253.3 15.7 %collective-permute-start.23 = (bf16[80,1024]{1,0:T(8,128)(2,1)S(1)}, bf16[80,1024]{1,0:T(8,128)(2,1)S(1)}, u32[]{:S(2)}, u32[]{:S(2)}) collective-permute-start(bf16[80,1024]{1,0:T(8,128)(2,1)S(1)} %get-tuple-element.61), channel_id=1, source_target_pairs={{0,7},{1,6},{2,5},{3,4},{4,3},{5,2},{6,1},{7,0},{8,15},{9,14},{10,... | collective-permute-start | bytes 491528 | tf_op jit(solution)/shard_map/ppermute | solution.py:405
  254.6 16.3 %collective-permute-start.53 = (bf16[40,1280]{1,0:T(8,128)(2,1)S(1)}, bf16[40,1280]{1,0:T(8,128)(2,1)S(1)}, u32[]{:S(2)}, u32[]{:S(2)}) collective-permute-start(bf16[40,1280]{1,0:T(8,128)(2,1)S(1)} %get-tuple-element.87.part), channel_id=1, source_target_pairs={{0,16},{16,0},{1,17},{17,1},{2,18},{18,2},{3,19},{19,3},{4,20},{20... | collective-permute-start | bytes 307208 | tf_op jit(solution)/shard_map/ppermute | solution.py:405
  (54 other events, 428.6 us)

commit v2 on v1

--- a/solution.py
+++ b/solution.py
@@ -31,14 +31,15 @@
 
 
 def head_kernel(
-    info_ref, begun_ref, turned_ref, par_ref, *refs,
+    info_ref, begun_ref, par_ref, turned_ref, turned_too_ref, *refs,
 ):
-    last_refs, refs = refs[:4], refs[4:]
+    last_refs, last_too_refs, refs = refs[:4], refs[4:8], refs[8:]
     pre_grad_ref, small_ref, pre_ref, slope_ref, sums_ref, center_ref, rstd_ref = refs
     ch, cells = pre_ref.shape
     width = ch // GROUPS
     count = width * cells
     add_product(begun_ref, turned_ref, last_refs, pre_ref)
+    add_product(pre_ref, turned_too_ref, last_too_refs, pre_ref)
 
     def at(g):
         return pl.ds(pl.multiple_of(g * width, 8), width)
@@ -134,12 +135,12 @@
     small_ref[...] = jnp.where(line == 3, margin * margin, turned * k)
 
 
-def head(sign, begun, turned, params, last):
+def head(sign, begun, params, turned, last):
     ch, cells = begun.shape
     return pl.pallas_call(
         head_kernel,
         out_shape=(jax.ShapeDtypeStruct((ch, cells), BF16), jax.ShapeDtypeStruct((EXTRA, ch), F32)),
-        in_specs=[SMEM] + [VMEM] * 7,
+        in_specs=[SMEM] + [VMEM] * 12,
         out_specs=(VMEM, VMEM),
         scratch_shapes=[pltpu.VMEM((ch, cells), F32)] * 2
         + [pltpu.VMEM((3, ch, 128), F32)]
@@ -149,7 +150,7 @@
         ),
         compiler_params=pltpu.CompilerParams(vmem_limit_bytes=28 << 20),
         name="head",
-    )(sign, begun, turned, params, *last)
+    )(sign, begun, params, *turned, *last)
 
 
 def add_product(begun_ref, turned_ref, refs, out_ref):
@@ -431,13 +432,13 @@
         image[m] = exchange(block, "mp", n, m) if m else block
     weights = gather_weight(conv_weight, at, n, row)
     pre = None
-    for k in PRODUCTS[:-1]:
+    for k in PRODUCTS[:2]:
         pre = product(pre, weights[k].T, [image[m] for m in SETS[k]])
         pre, params = lax.optimization_barrier((pre, params))
     twin = [exchange(image[m], "mp", n, 1) for m in bit_order(1)]
-    k = PRODUCTS[-1]
-    last = [image[m] for m in SETS[k]]
-    grad_pre, small = head(2 * labels - 1, pre, weights[k].T, params, last)
+    turned = [weights[k].T for k in PRODUCTS[2:]]
+    last = [image[m] for k in PRODUCTS[2:] for m in SETS[k]]
+    grad_pre, small = head(2 * labels - 1, pre, params, turned, last)
     twin_pre = exchange(grad_pre, "mp", n, 1)
     twin_small = exchange(small, "mp", n, 1)
     blocks = {}

time: 273 us -> 278 us (1.018)
  local copies, waits for them, and re-layouts: 35.8 us -> 40.7 us
  starting transfers between devices: 61.7 us -> 66.4 us
  Pallas kernels: 38.8 us -> 35.1 us
    ppermute x54, starting transfers between devices: 61.7 us -> 66.4 us  [exchange(): return lax.ppermute(value, axis, [(i, i ^ mask) for i in range(size)])]
    unnamed x68 -> x86, local copies, waits for them, and re-layouts: 25.6 us -> 30 us
    pallas_call x3 -> x2, Pallas kernels: 7.36 us -> 3.4 us  [product(): pl.pallas_call(first_kernel if begun is None else next_kernel, out_shape=...]
  transfers between devices with their start and end apart: 54 -> 54, of which waited for: 23 -> 23; matrix products, arithmetic and copies ran while one was open for 4% -> 4% of each run, Pallas kernels for 9% -> 7%
where the time goes in v2:
time: 278 us; the launch traced here: 277 us
  waiting for transfers between devices  133 us (48%)
  starting transfers between devices  66.4 us (24%)
  local copies, waits for them, and re-layouts  40.7 us (15%)
  Pallas kernels  35.1 us (13%)
    ppermute x54, waiting for transfers between devices, exchange(): return lax.ppermute(value, axis, [(i, i ^ mask) for i in range(size)])  133 us
    ppermute x54, starting transfers between devices, exchange(): return lax.ppermute(value, axis, [(i, i ^ mask) for i in range(size)])  66.4 us
    unnamed x86, local copies, waits for them, and re-layouts  30 us
    pallas_call x10, Pallas kernels, local(): pl.pallas_call(kernel, out_shape=outs, in_specs=specs, cost_estimate=pl.C...  13.3 us
    pallas_call x1, Pallas kernels, head(): pl.pallas_call(head_kernel, out_shape=(jax.ShapeDtypeStruct((ch, cells),...  11.5 us
  transfers between devices with their start and end apart: 54, of which 23 were waited for; matrix products, arithmetic and copies ran while one was open for 4% of the time, Pallas kernels for 7%

profile of v2, /device:TPU:12, one launch (start us, length us, event | category | flops | bytes accessed | tf_op | source)
XLA Modules:
  0.0 277.2 jit_solution(9953096321786260479)
XLA Ops:
  2.2 2.6 collective-permute-start
  4.8 4.2 %collective-permute-done = bf16[1,80,640]{2,1,0:T(8,128)(2,1)S(1)} collective-permute-done((bf16[1,80,640]{2,1,0:T(8,128)(2,1)S(1)}, bf16[1,80,640]{2,1,0:T(8,128)(2,1)S(1)}, u32[]{:S(2)}, u32[]{:S(2)}) %collective-permute-start) | collective-permute-done | bytes 102432 | tf_op jit(solution)/shard_map/ppermute | solution.py:406
  10.5 5.6 %collective-permute-done.1 = bf16[2,80,640]{2,1,0:T(8,128)(2,1)S(1)} collective-permute-done((bf16[2,80,640]{2,1,0:T(8,128)(2,1)S(1)}, bf16[2,80,640]{2,1,0:T(8,128)(2,1)S(1)}, u32[]{:S(2)}, u32[]{:S(2)}) %collective-permute-start.1) | collective-permute-done | bytes 204832 | tf_op jit(solution)/shard_map/ppermute | solution.py:406
  17.7 9.0 %collective-permute-done.2 = bf16[4,80,640]{2,1,0:T(8,128)(2,1)S(1)} collective-permute-done((bf16[4,80,640]{2,1,0:T(8,128)(2,1)S(1)}, bf16[4,80,640]{2,1,0:T(8,128)(2,1)S(1)}, u32[]{:S(2)}, u32[]{:S(2)}) %collective-permute-start.2) | collective-permute-done | bytes 409632 | tf_op jit(solution)/shard_map/ppermute | solution.py:406
  29.6 15.8 %collective-permute-done.3.across_ref = bf16[8,80,640]{2,1,0:T(8,128)(2,1)S(1)} collective-permute-done((bf16[8,80,640]{2,1,0:T(8,128)(2,1)S(1)}, bf16[8,80,640]{2,1,0:T(8,128)(2,1)S(1)}, u32[]{:S(2)}, u32[]{:S(2)}) %collective-permute-start.3) | collective-permute-done | bytes 819232 | tf_op jit(solution)/shard_map/ppermute | solution.py:406
  46.4 2.8 %dynamic-slice_bitcast_fusion = (bf16[80,1024]{1,0:T(8,128)(2,1)}, bf16[80,1024]{1,0:T(8,128)(2,1)}, bf16[80,1024]{1,0:T(8,128)(2,1)}, bf16[80,1024]{1,0:T(8,128...) fusion(bf16[16,80,1024]{2,1,0:T(8,128)(2,1)} %param.6, ...), kind=kLoop, calls=%fused_computation.3 | loop fusion | bytes 5242944 | tf_op jit(solution)/shard_map/jit(dynamic_index_in_dim)/squeeze | solution.py:431
  49.2 2.8 collective-permute-start.5
  52.6 2.4 collective-permute-start.7
  56.1 14.9 %collective-permute-done.5.refs_0_.refs_6_ = bf16[80,1024]{1,0:T(8,128)(2,1)S(1)} collective-permute-done((bf16[80,1024]{1,0:T(8,128)(2,1)S(1)}, bf16[80,1024]{1,0:T(8,128)(2,1)S(1)}, u32[]{:S(2)}, u32[]{:S(2)}) %collective-permute-start.5) | collective-permute-done | bytes 163872 | tf_op jit(solution)/shard_map/ppermute | solution.py:406
  71.7 2.4 collective-permute-done.6.refs_1_.refs_4_
  74.8 2.8 %collective-permute-done.7.refs_2_ = bf16[80,1024]{1,0:T(8,128)(2,1)S(1)} collective-permute-done((bf16[80,1024]{1,0:T(8,128)(2,1)S(1)}, bf16[80,1024]{1,0:T(8,128)(2,1)S(1)}, u32[]{:S(2)}, u32[]{:S(2)}) %collective-permute-start.7) | collective-permute-done | bytes 163872 | tf_op jit(solution)/shard_map/ppermute | solution.py:406
  83.2 4.1 %collective-permute-start.13 = (bf16[80,1024]{1,0:T(8,128)(2,1)S(1)}, bf16[80,1024]{1,0:T(8,128)(2,1)S(1)}, u32[]{:S(2)}, u32[]{:S(2)}) collective-permute-start(bf16[80,1024]{1,0:T(8,128)(2,1)S(1)} %get-tuple-element.93), channel_id=1, source_target_pairs={{0,10},{1,11},{2,8},{3,9},{4,14},{5,15},{6,12},{7,13},{8,2},{9,3},... | collective-permute-start | bytes 491528 | tf_op jit(solution)/shard_map/ppermute | solution.py:406
  90.2 5.3 %collective-permute-done.12.refs_0_.refs_7_ = bf16[80,1024]{1,0:T(8,128)(2,1)S(1)} collective-permute-done((bf16[80,1024]{1,0:T(8,128)(2,1)S(1)}, bf16[80,1024]{1,0:T(8,128)(2,1)S(1)}, u32[]{:S(2)}, u32[]{:S(2)}) %collective-permute-start.12) | collective-permute-done | bytes 163872 | tf_op jit(solution)/shard_map/ppermute | solution.py:406
  96.2 4.5 %collective-permute-done.13.refs_1_.refs_5_ = bf16[80,1024]{1,0:T(8,128)(2,1)S(1)} collective-permute-done((bf16[80,1024]{1,0:T(8,128)(2,1)S(1)}, bf16[80,1024]{1,0:T(8,128)(2,1)S(1)}, u32[]{:S(2)}, u32[]{:S(2)}) %collective-permute-start.13) | collective-permute-done | bytes 163872 | tf_op jit(solution)/shard_map/ppermute | solution.py:406
  101.3 3.8 %collective-permute-start.17 = (bf16[80,1024]{1,0:T(8,128)(2,1)}, bf16[80,1024]{1,0:T(8,128)(2,1)}, u32[]{:S(2)}, u32[]{:S(2)}) collective-permute-start(bf16[80,1024]{1,0:T(8,128)(2,1)} %get-tuple-element.89), channel_id=1, source_target_pairs={{0,11},{1,10},{2,9},{3,8},{4,15},{5,14},{6,13},{7,12},{8,3},{9,2},... | collective-permute-start | bytes 491528 | tf_op jit(solution)/shard_map/ppermute | solution.py:406
  107.4 2.4 collective-permute-start.19
  123.6 2.5 copy-done.1
  132.3 2.5 copy-done.3
  140.3 11.5 %head.1 = (bf16[1280,1024]{1,0:T(8,128)(2,1)S(1)}, f32[8,1280]{1,0:T(8,128)S(1)}) custom-call(s32[1]{0:T(128)S(6)} %sub.3.info_ref, f32[1280,1024]{1,0:T(8,128)S(1)} %copy-done.3, f32[3,1280,128]{2,1,0:T(8,128)S(1)} %copy-done.8, bf16[1280,320]{1,0:T(8,128)(2,1)S(1)} %bitcast.44, bf16[1280,320]{1,0:T(8,128)(2,1)S(1)} %bitcast.45, ...), custom_call_target="tpu_custom_call" | custom-call | flops 5033164800 | bytes 10485760 | tf_op jit(solution)/shard_map/head/pallas_call | solution.py:140
  153.2 3.9 %collective-permute-done.39.refs_0_ = bf16[80,1024]{1,0:T(8,128)(2,1)S(1)} collective-permute-done((bf16[80,1024]{1,0:T(8,128)(2,1)S(1)}, bf16[80,1024]{1,0:T(8,128)(2,1)S(1)}, u32[]{:S(2)}, u32[]{:S(2)}) %collective-permute-start.39) | collective-permute-done | bytes 163872 | tf_op jit(solution)/shard_map/ppermute | solution.py:406
  158.7 2.8 %weight_keep.1.own_ref = f32[640,1280]{1,0:T(8,128)S(1)} custom-call(bf16[1280,1024]{1,0:T(8,128)(2,1)S(1)} %get-tuple-element.53.pre_grad_ref, bf16[80,1024]{1,0:T(8,128)(2,1)S(1)} %get-tuple-element.95.refs_3_.refs_0_, bf16[80,1024]{1,0:T(8,128)(2,1)S(1)} %copy-done.34, bf16[80,1024]{1,0:T(8,128)(2,1)S(1)} %copy-done.19, ...), custom_call_target="tpu_custom_call" | custom-call | flops 1677721600 | bytes 5242880 | tf_op jit(solution)/shard_map/weight_keep/pallas_call | solution.py:220
  161.6 2.6 shard_map.97
  165.3 19.7 %collective-permute-done.48.qb = f32[320,640]{1,0:T(8,128)S(1)} collective-permute-done((f32[320,640]{1,0:T(8,128)S(1)}, f32[320,640]{1,0:T(8,128)S(1)}, u32[]{:S(2)}, u32[]{:S(2)}) %collective-permute-start.48) | collective-permute-done | bytes 819232 | tf_op jit(solution)/shard_map/ppermute | solution.py:406
  187.8 9.2 %collective-permute-done.50.qb = f32[160,640]{1,0:T(8,128)S(1)} collective-permute-done((f32[160,640]{1,0:T(8,128)S(1)}, f32[160,640]{1,0:T(8,128)S(1)}, u32[]{:S(2)}, u32[]{:S(2)}) %collective-permute-start.50) | collective-permute-done | bytes 409632 | tf_op jit(solution)/shard_map/ppermute | solution.py:406
  200.7 2.7 collective-permute-start.34
  206.6 10.6 %collective-permute-start.26 = (bf16[80,1024]{1,0:T(8,128)(2,1)S(1)}, bf16[80,1024]{1,0:T(8,128)(2,1)S(1)}, u32[]{:S(2)}, u32[]{:S(2)}) collective-permute-start(bf16[80,1024]{1,0:T(8,128)(2,1)S(1)} %get-tuple-element.60), channel_id=1, source_target_pairs={{0,4},{1,5},{2,6},{3,7},{4,0},{5,1},{6,2},{7,3},{8,12},{9,13},{10,... | collective-permute-start | bytes 491528 | tf_op jit(solution)/shard_map/ppermute | solution.py:406
  217.2 2.6 collective-permute-done.34.refs_2_
  219.8 5.9 %collective-permute-done.35.refs_3_ = bf16[80,1024]{1,0:T(8,128)(2,1)S(1)} collective-permute-done((bf16[80,1024]{1,0:T(8,128)(2,1)S(1)}, bf16[80,1024]{1,0:T(8,128)(2,1)S(1)}, u32[]{:S(2)}, u32[]{:S(2)}) %collective-permute-start.35) | collective-permute-done | bytes 163872 | tf_op jit(solution)/shard_map/ppermute | solution.py:406
  234.4 13.6 %collective-permute-done.29 = bf16[80,1024]{1,0:T(8,128)(2,1)S(1)} collective-permute-done((bf16[80,1024]{1,0:T(8,128)(2,1)S(1)}, bf16[80,1024]{1,0:T(8,128)(2,1)S(1)}, u32[]{:S(2)}, u32[]{:S(2)}) %collective-permute-start.29) | collective-permute-done | bytes 163872 | tf_op jit(solution)/shard_map/ppermute | solution.py:406
  252.0 6.4 %collective-permute-start.21 = (bf16[80,1024]{1,0:T(8,128)(2,1)S(1)}, bf16[80,1024]{1,0:T(8,128)(2,1)S(1)}, u32[]{:S(2)}, u32[]{:S(2)}) collective-permute-start(bf16[80,1024]{1,0:T(8,128)(2,1)S(1)} %get-tuple-element.55), channel_id=1, source_target_pairs={{0,11},{1,10},{2,9},{3,8},{4,15},{5,14},{6,13},{7,12},{8,3},{9,2},... | collective-permute-start | bytes 491528 | tf_op jit(solution)/shard_map/ppermute | solution.py:406
  264.4 4.7 %collective-permute-done.20.refs_0_ = bf16[80,1024]{1,0:T(8,128)(2,1)S(1)} collective-permute-done((bf16[80,1024]{1,0:T(8,128)(2,1)S(1)}, bf16[80,1024]{1,0:T(8,128)(2,1)S(1)}, u32[]{:S(2)}, u32[]{:S(2)}) %collective-permute-start.20) | collective-permute-done | bytes 163872 | tf_op jit(solution)/shard_map/ppermute | solution.py:406
  270.4 3.6 %collective-permute-done.23.refs_3_ = bf16[80,1024]{1,0:T(8,128)(2,1)S(1)} collective-permute-done((bf16[80,1024]{1,0:T(8,128)(2,1)S(1)}, bf16[80,1024]{1,0:T(8,128)(2,1)S(1)}, u32[]{:S(2)}, u32[]{:S(2)}) %collective-permute-start.23) | collective-permute-done | bytes 163872 | tf_op jit(solution)/shard_map/ppermute | solution.py:406
  (195 shorter events, 85.0 us)
Async XLA Ops:
  26.9 18.5 %collective-permute-start.3 = (bf16[8,80,640]{2,1,0:T(8,128)(2,1)S(1)}, bf16[8,80,640]{2,1,0:T(8,128)(2,1)S(1)}, u32[]{:S(2)}, u32[]{:S(2)}) collective-permute-start(bf16[8,80,640]{2,1,0:T(8,128)(2,1)S(1)} %pad_maximum_fusion.near_ref), channel_id=1, source_target_pairs={{0,16},{16,0},{1,17},{17,1},{2,18},{18,2},{3,19},{19,3},{4,20},{20... | collective-permute-start | bytes 2457608 | tf_op jit(solution)/shard_map/ppermute | solution.py:406
  46.3 59.9 %collective-permute-start.4 = (bf16[16,80,640]{2,1,0:T(8,128)(2,1)}, bf16[16,80,640]{2,1,0:T(8,128)(2,1)S(1)}, u32[]{:S(2)}, u32[]{:S(2)}) collective-permute-start(bf16[16,80,640]{2,1,0:T(8,128)(2,1)} %constant_dynamic-update-slice_fusion), channel_id=1, source_target_pairs={{0,1},{1,0},{2,3},{3,2},{4,5},{5,4},{6,7},{7,6},{8,9},{9,8},{10,11... | collective-permute-start | bytes 4915208 | tf_op jit(solution)/shard_map/ppermute | solution.py:406
  49.2 21.9 %collective-permute-start.5 = (bf16[80,1024]{1,0:T(8,128)(2,1)S(1)}, bf16[80,1024]{1,0:T(8,128)(2,1)S(1)}, u32[]{:S(2)}, u32[]{:S(2)}) collective-permute-start(bf16[80,1024]{1,0:T(8,128)(2,1)S(1)} %get-tuple-element.102), channel_id=1, source_target_pairs={{0,12},{1,13},{2,14},{3,15},{4,8},{5,9},{6,10},{7,11},{8,4},{9,5},... | collective-permute-start | bytes 491528 | tf_op jit(solution)/shard_map/ppermute | solution.py:406
  52.0 22.1 %collective-permute-start.6 = (bf16[80,1024]{1,0:T(8,128)(2,1)S(1)}, bf16[80,1024]{1,0:T(8,128)(2,1)S(1)}, u32[]{:S(2)}, u32[]{:S(2)}) collective-permute-start(bf16[80,1024]{1,0:T(8,128)(2,1)S(1)} %get-tuple-element.101), channel_id=1, source_target_pairs={{0,8},{1,9},{2,10},{3,11},{4,12},{5,13},{6,14},{7,15},{8,0},{9,1},... | collective-permute-start | bytes 491528 | tf_op jit(solution)/shard_map/ppermute | solution.py:406
  52.6 25.0 %collective-permute-start.7 = (bf16[80,1024]{1,0:T(8,128)(2,1)S(1)}, bf16[80,1024]{1,0:T(8,128)(2,1)S(1)}, u32[]{:S(2)}, u32[]{:S(2)}) collective-permute-start(bf16[80,1024]{1,0:T(8,128)(2,1)S(1)} %get-tuple-element.100), channel_id=1, source_target_pairs={{0,13},{1,12},{2,15},{3,14},{4,9},{5,8},{6,11},{7,10},{8,5},{9,4},... | collective-permute-start | bytes 491528 | tf_op jit(solution)/shard_map/ppermute | solution.py:406
  55.0 25.6 %collective-permute-start.8 = (bf16[80,1024]{1,0:T(8,128)(2,1)S(1)}, bf16[80,1024]{1,0:T(8,128)(2,1)S(1)}, u32[]{:S(2)}, u32[]{:S(2)}) collective-permute-start(bf16[80,1024]{1,0:T(8,128)(2,1)S(1)} %get-tuple-element.99), channel_id=1, source_target_pairs={{0,9},{1,8},{2,11},{3,10},{4,13},{5,12},{6,15},{7,14},{8,1},{9,0},... | collective-permute-start | bytes 491528 | tf_op jit(solution)/shard_map/ppermute | solution.py:406
  74.8 12.5 %collective-permute-start.11 = (bf16[80,1024]{1,0:T(8,128)(2,1)S(1)}, bf16[80,1024]{1,0:T(8,128)(2,1)S(1)}, u32[]{:S(2)}, u32[]{:S(2)}) collective-permute-start(bf16[80,1024]{1,0:T(8,128)(2,1)S(1)} %get-tuple-element.96), channel_id=1, source_target_pairs={{0,1},{1,0},{2,3},{3,2},{4,5},{5,4},{6,7},{7,6},{8,9},{9,8},{10,11... | collective-permute-start | bytes 491528 | tf_op jit(solution)/shard_map/ppermute | solution.py:406
  81.3 14.2 %collective-permute-start.12 = (bf16[80,1024]{1,0:T(8,128)(2,1)S(1)}, bf16[80,1024]{1,0:T(8,128)(2,1)S(1)}, u32[]{:S(2)}, u32[]{:S(2)}) collective-permute-start(bf16[80,1024]{1,0:T(8,128)(2,1)S(1)} %get-tuple-element.94), channel_id=1, source_target_pairs={{0,14},{1,15},{2,12},{3,13},{4,10},{5,11},{6,8},{7,9},{8,6},{9,7},... | collective-permute-start | bytes 491528 | tf_op jit(solution)/shard_map/ppermute | solution.py:406
  83.2 17.5 %collective-permute-start.13 = (bf16[80,1024]{1,0:T(8,128)(2,1)S(1)}, bf16[80,1024]{1,0:T(8,128)(2,1)S(1)}, u32[]{:S(2)}, u32[]{:S(2)}) collective-permute-start(bf16[80,1024]{1,0:T(8,128)(2,1)S(1)} %get-tuple-element.93), channel_id=1, source_target_pairs={{0,10},{1,11},{2,8},{3,9},{4,14},{5,15},{6,12},{7,13},{8,2},{9,3},... | collective-permute-start | bytes 491528 | tf_op jit(solution)/shard_map/ppermute | solution.py:406
  88.0 17.1 %collective-permute-start.14 = (bf16[80,1024]{1,0:T(8,128)(2,1)S(1)}, bf16[80,1024]{1,0:T(8,128)(2,1)S(1)}, u32[]{:S(2)}, u32[]{:S(2)}) collective-permute-start(bf16[80,1024]{1,0:T(8,128)(2,1)S(1)} %get-tuple-element.92), channel_id=1, source_target_pairs={{0,2},{1,3},{2,0},{3,1},{4,6},{5,7},{6,4},{7,5},{8,10},{9,11},{10,... | collective-permute-start | bytes 491528 | tf_op jit(solution)/shard_map/ppermute | solution.py:406
  90.2 42.1 %collective-permute-start.15 = (bf16[80,1024]{1,0:T(8,128)(2,1)}, bf16[80,1024]{1,0:T(8,128)(2,1)}, u32[]{:S(2)}, u32[]{:S(2)}) collective-permute-start(bf16[80,1024]{1,0:T(8,128)(2,1)} %get-tuple-element.91), channel_id=1, source_target_pairs={{0,3},{1,2},{2,1},{3,0},{4,7},{5,6},{6,5},{7,4},{8,11},{9,10},{10,... | collective-permute-start | bytes 491528 | tf_op jit(solution)/shard_map/ppermute | solution.py:406
  96.2 36.1 %collective-permute-start.16 = (bf16[80,1024]{1,0:T(8,128)(2,1)}, bf16[80,1024]{1,0:T(8,128)(2,1)}, u32[]{:S(2)}, u32[]{:S(2)}) collective-permute-start(bf16[80,1024]{1,0:T(8,128)(2,1)} %get-tuple-element.90), channel_id=1, source_target_pairs={{0,15},{1,14},{2,13},{3,12},{4,11},{5,10},{6,9},{7,8},{8,7},{9,6},... | collective-permute-start | bytes 491528 | tf_op jit(solution)/shard_map/ppermute | solution.py:406
  101.3 31.0 %collective-permute-start.17 = (bf16[80,1024]{1,0:T(8,128)(2,1)}, bf16[80,1024]{1,0:T(8,128)(2,1)}, u32[]{:S(2)}, u32[]{:S(2)}) collective-permute-start(bf16[80,1024]{1,0:T(8,128)(2,1)} %get-tuple-element.89), channel_id=1, source_target_pairs={{0,11},{1,10},{2,9},{3,8},{4,15},{5,14},{6,13},{7,12},{8,3},{9,2},... | collective-permute-start | bytes 491528 | tf_op jit(solution)/shard_map/ppermute | solution.py:406
  105.8 26.5 %collective-permute-start.18 = (bf16[80,1024]{1,0:T(8,128)(2,1)}, bf16[80,1024]{1,0:T(8,128)(2,1)}, u32[]{:S(2)}, u32[]{:S(2)}) collective-permute-start(bf16[80,1024]{1,0:T(8,128)(2,1)} %get-tuple-element.103), channel_id=1, source_target_pairs={{0,6},{1,7},{2,4},{3,5},{4,2},{5,3},{6,0},{7,1},{8,14},{9,15},{10,... | collective-permute-start | bytes 491528 | tf_op jit(solution)/shard_map/ppermute | solution.py:406
  107.4 24.9 %collective-permute-start.19 = (bf16[80,1024]{1,0:T(8,128)(2,1)}, bf16[80,1024]{1,0:T(8,128)(2,1)}, u32[]{:S(2)}, u32[]{:S(2)}) collective-permute-start(bf16[80,1024]{1,0:T(8,128)(2,1)} %get-tuple-element.88), channel_id=1, source_target_pairs={{0,7},{1,6},{2,5},{3,4},{4,3},{5,2},{6,1},{7,0},{8,15},{9,14},{10,... | collective-permute-start | bytes 491528 | tf_op jit(solution)/shard_map/ppermute | solution.py:406
  164.2 21.0 %collective-permute-start.47 = (f32[328,640]{1,0:T(8,128)S(1)}, f32[328,640]{1,0:T(8,128)S(1)}, u32[]{:S(2)}, u32[]{:S(2)}) collective-permute-start(f32[328,640]{1,0:T(8,128)S(1)} %get-tuple-element.72), channel_id=1, source_target_pairs={{0,16},{16,0},{1,17},{17,1},{2,18},{18,2},{3,19},{19,3},{4,20},{20... | collective-permute-start | bytes 2519048 | tf_op jit(solution)/shard_map/ppermute | solution.py:406
  164.8 20.2 %collective-permute-start.48 = (f32[320,640]{1,0:T(8,128)S(1)}, f32[320,640]{1,0:T(8,128)S(1)}, u32[]{:S(2)}, u32[]{:S(2)}) collective-permute-start(f32[320,640]{1,0:T(8,128)S(1)} %get-tuple-element.74), channel_id=1, source_target_pairs={{0,2},{1,3},{2,0},{3,1},{4,6},{5,7},{6,4},{7,5},{8,10},{9,11},{10,... | collective-permute-start | bytes 2457608 | tf_op jit(solution)/shard_map/ppermute | solution.py:406
  197.8 31.6 %collective-permute-start.51 = (f32[88,1280]{1,0:T(8,128)S(1)}, f32[88,1280]{1,0:T(8,128)S(1)}, u32[]{:S(2)}, u32[]{:S(2)}) collective-permute-start(f32[88,1280]{1,0:T(8,128)S(1)} %get-tuple-element.80), channel_id=1, source_target_pairs={{0,4},{1,5},{2,6},{3,7},{4,0},{5,1},{6,2},{7,3},{8,12},{9,13},{10,... | collective-permute-start | bytes 1351688 | tf_op jit(solution)/shard_map/ppermute | solution.py:406
  200.7 19.2 %collective-permute-start.34 = (bf16[80,1024]{1,0:T(8,128)(2,1)S(1)}, bf16[80,1024]{1,0:T(8,128)(2,1)S(1)}, u32[]{:S(2)}, u32[]{:S(2)}) collective-permute-start(bf16[80,1024]{1,0:T(8,128)(2,1)S(1)} %get-tuple-element.67), channel_id=1, source_target_pairs={{0,8},{1,9},{2,10},{3,11},{4,12},{5,13},{6,14},{7,15},{8,0},{9,1},... | collective-permute-start | bytes 491528 | tf_op jit(solution)/shard_map/ppermute | solution.py:406
  203.4 22.4 %collective-permute-start.35 = (bf16[80,1024]{1,0:T(8,128)(2,1)S(1)}, bf16[80,1024]{1,0:T(8,128)(2,1)S(1)}, u32[]{:S(2)}, u32[]{:S(2)}) collective-permute-start(bf16[80,1024]{1,0:T(8,128)(2,1)S(1)} %get-tuple-element.68), channel_id=1, source_target_pairs={{0,13},{1,12},{2,15},{3,14},{4,9},{5,8},{6,11},{7,10},{8,5},{9,4},... | collective-permute-start | bytes 491528 | tf_op jit(solution)/shard_map/ppermute | solution.py:406
  203.4 25.2 %collective-permute-start.36 = (bf16[80,1024]{1,0:T(8,128)(2,1)S(1)}, bf16[80,1024]{1,0:T(8,128)(2,1)S(1)}, u32[]{:S(2)}, u32[]{:S(2)}) collective-permute-start(bf16[80,1024]{1,0:T(8,128)(2,1)S(1)} %get-tuple-element.69), channel_id=1, source_target_pairs={{0,9},{1,8},{2,11},{3,10},{4,13},{5,12},{6,15},{7,14},{8,1},{9,0},... | collective-permute-start | bytes 491528 | tf_op jit(solution)/shard_map/ppermute | solution.py:406
  206.6 25.2 %collective-permute-start.26 = (bf16[80,1024]{1,0:T(8,128)(2,1)S(1)}, bf16[80,1024]{1,0:T(8,128)(2,1)S(1)}, u32[]{:S(2)}, u32[]{:S(2)}) collective-permute-start(bf16[80,1024]{1,0:T(8,128)(2,1)S(1)} %get-tuple-element.60), channel_id=1, source_target_pairs={{0,4},{1,5},{2,6},{3,7},{4,0},{5,1},{6,2},{7,3},{8,12},{9,13},{10,... | collective-permute-start | bytes 491528 | tf_op jit(solution)/shard_map/ppermute | solution.py:406
  219.8 13.2 %collective-permute-start.27 = (bf16[80,1024]{1,0:T(8,128)(2,1)S(1)}, bf16[80,1024]{1,0:T(8,128)(2,1)S(1)}, u32[]{:S(2)}, u32[]{:S(2)}) collective-permute-start(bf16[80,1024]{1,0:T(8,128)(2,1)S(1)} %get-tuple-element.61), channel_id=1, source_target_pairs={{0,5},{1,4},{2,7},{3,6},{4,1},{5,0},{6,3},{7,2},{8,13},{9,12},{10,... | collective-permute-start | bytes 491528 | tf_op jit(solution)/shard_map/ppermute | solution.py:406
  228.6 19.4 %collective-permute-start.29 = (bf16[80,1024]{1,0:T(8,128)(2,1)S(1)}, bf16[80,1024]{1,0:T(8,128)(2,1)S(1)}, u32[]{:S(2)}, u32[]{:S(2)}) collective-permute-start(bf16[80,1024]{1,0:T(8,128)(2,1)S(1)} %get-tuple-element.63), channel_id=1, source_target_pairs={{0,12},{1,13},{2,14},{3,15},{4,8},{5,9},{6,10},{7,11},{8,4},{9,5},... | collective-permute-start | bytes 491528 | tf_op jit(solution)/shard_map/ppermute | solution.py:406
  229.5 20.4 %collective-permute-start.31 = (bf16[80,1024]{1,0:T(8,128)(2,1)S(1)}, bf16[80,1024]{1,0:T(8,128)(2,1)S(1)}, u32[]{:S(2)}, u32[]{:S(2)}) collective-permute-start(bf16[80,1024]{1,0:T(8,128)(2,1)S(1)} %get-tuple-element.64), channel_id=1, source_target_pairs={{0,8},{1,9},{2,10},{3,11},{4,12},{5,13},{6,14},{7,15},{8,0},{9,1},... | collective-permute-start | bytes 491528 | tf_op jit(solution)/shard_map/ppermute | solution.py:406
  231.8 26.6 %collective-permute-start.52 = (f32[48,1280]{1,0:T(8,128)S(1)}, f32[48,1280]{1,0:T(8,128)S(1)}, u32[]{:S(2)}, u32[]{:S(2)}) collective-permute-start(f32[48,1280]{1,0:T(8,128)S(1)} %get-tuple-element.82), channel_id=1, source_target_pairs={{0,8},{1,9},{2,10},{3,11},{4,12},{5,13},{6,14},{7,15},{8,0},{9,1},... | collective-permute-start | bytes 737288 | tf_op jit(solution)/shard_map/ppermute | solution.py:406
  233.1 18.8 %collective-permute-start.24 = (bf16[80,1024]{1,0:T(8,128)(2,1)S(1)}, bf16[80,1024]{1,0:T(8,128)(2,1)S(1)}, u32[]{:S(2)}, u32[]{:S(2)}) collective-permute-start(bf16[80,1024]{1,0:T(8,128)(2,1)S(1)} %get-tuple-element.58), channel_id=1, source_target_pairs={{0,2},{1,3},{2,0},{3,1},{4,6},{5,7},{6,4},{7,5},{8,10},{9,11},{10,... | collective-permute-start | bytes 491528 | tf_op jit(solution)/shard_map/ppermute | solution.py:406
  234.1 17.9 %collective-permute-start.25 = (bf16[80,1024]{1,0:T(8,128)(2,1)S(1)}, bf16[80,1024]{1,0:T(8,128)(2,1)S(1)}, u32[]{:S(2)}, u32[]{:S(2)}) collective-permute-start(bf16[80,1024]{1,0:T(8,128)(2,1)S(1)} %get-tuple-element.59), channel_id=1, source_target_pairs={{0,3},{1,2},{2,1},{3,0},{4,7},{5,6},{6,5},{7,4},{8,11},{9,10},{10,... | collective-permute-start | bytes 491528 | tf_op jit(solution)/shard_map/ppermute | solution.py:406
  251.9 17.1 %collective-permute-start.20 = (bf16[80,1024]{1,0:T(8,128)(2,1)S(1)}, bf16[80,1024]{1,0:T(8,128)(2,1)S(1)}, u32[]{:S(2)}, u32[]{:S(2)}) collective-permute-start(bf16[80,1024]{1,0:T(8,128)(2,1)S(1)} %get-tuple-element.54), channel_id=1, source_target_pairs={{0,15},{1,14},{2,13},{3,12},{4,11},{5,10},{6,9},{7,8},{8,7},{9,6},... | collective-permute-start | bytes 491528 | tf_op jit(solution)/shard_map/ppermute | solution.py:406
  252.0 18.4 %collective-permute-start.21 = (bf16[80,1024]{1,0:T(8,128)(2,1)S(1)}, bf16[80,1024]{1,0:T(8,128)(2,1)S(1)}, u32[]{:S(2)}, u32[]{:S(2)}) collective-permute-start(bf16[80,1024]{1,0:T(8,128)(2,1)S(1)} %get-tuple-element.55), channel_id=1, source_target_pairs={{0,11},{1,10},{2,9},{3,8},{4,15},{5,14},{6,13},{7,12},{8,3},{9,2},... | collective-permute-start | bytes 491528 | tf_op jit(solution)/shard_map/ppermute | solution.py:406
  258.4 15.6 %collective-permute-start.23 = (bf16[80,1024]{1,0:T(8,128)(2,1)S(1)}, bf16[80,1024]{1,0:T(8,128)(2,1)S(1)}, u32[]{:S(2)}, u32[]{:S(2)}) collective-permute-start(bf16[80,1024]{1,0:T(8,128)(2,1)S(1)} %get-tuple-element.57), channel_id=1, source_target_pairs={{0,7},{1,6},{2,5},{3,4},{4,3},{5,2},{6,1},{7,0},{8,15},{9,14},{10,... | collective-permute-start | bytes 491528 | tf_op jit(solution)/shard_map/ppermute | solution.py:406
  259.7 16.1 %collective-permute-start.53 = (bf16[40,1280]{1,0:T(8,128)(2,1)S(1)}, bf16[40,1280]{1,0:T(8,128)(2,1)S(1)}, u32[]{:S(2)}, u32[]{:S(2)}) collective-permute-start(bf16[40,1280]{1,0:T(8,128)(2,1)S(1)} %get-tuple-element.83.part), channel_id=1, source_target_pairs={{0,16},{16,0},{1,17},{17,1},{2,18},{18,2},{3,19},{19,3},{4,20},{20... | collective-permute-start | bytes 307208 | tf_op jit(solution)/shard_map/ppermute | solution.py:406
  (63 other events, 405.3 us)

commit v3 on v2

--- a/solution.py
+++ b/solution.py
@@ -31,15 +31,15 @@
 
 
 def head_kernel(
-    info_ref, begun_ref, par_ref, turned_ref, turned_too_ref, *refs,
+    info_ref, begun_ref, par_ref, weight_ref, weight_too_ref, *refs,
 ):
     last_refs, last_too_refs, refs = refs[:4], refs[4:8], refs[8:]
     pre_grad_ref, small_ref, pre_ref, slope_ref, sums_ref, center_ref, rstd_ref = refs
     ch, cells = pre_ref.shape
     width = ch // GROUPS
     count = width * cells
-    add_product(begun_ref, turned_ref, last_refs, pre_ref)
-    add_product(pre_ref, turned_too_ref, last_too_refs, pre_ref)
+    add_product(begun_ref, weight_ref, last_refs, pre_ref)
+    add_product(pre_ref, weight_too_ref, last_too_refs, pre_ref)
 
     def at(g):
         return pl.ds(pl.multiple_of(g * width, 8), width)
@@ -153,25 +153,27 @@
     )(sign, begun, params, *turned, *last)
 
 
-def add_product(begun_ref, turned_ref, refs, out_ref):
+def add_product(begun_ref, weight_ref, refs, out_ref):
     image = stacked(refs)
-    step = out_ref.shape[0] // 4
-    for j in range(4):
+    step = out_ref.shape[0] // 2
+    for j in range(2):
         rows = pl.ds(j * step, step)
-        product = jnp.dot(turned_ref[rows, :], image, preferred_element_type=F32)
+        product = lax.dot_general(
+            weight_ref[:, rows], image, (((0,), (0,)), ((), ())), preferred_element_type=F32
+        )
         out_ref[rows, :] = product if begun_ref is None else begun_ref[rows, :] + product
 
 
-def first_kernel(turned_ref, *refs):
-    add_product(None, turned_ref, refs[:-1], refs[-1])
-
-
-def next_kernel(begun_ref, turned_ref, *refs):
-    add_product(begun_ref, turned_ref, refs[:-1], refs[-1])
+def first_kernel(weight_ref, *refs):
+    add_product(None, weight_ref, refs[:-1], refs[-1])
+
+
+def next_kernel(begun_ref, weight_ref, *refs):
+    add_product(begun_ref, weight_ref, refs[:-1], refs[-1])
 
 
 def product(begun, turned, images):
-    ch, depth = turned.shape
+    depth, ch = turned.shape
     cells = images[0].shape[1]
     args = ([] if begun is None else [begun]) + [turned, *images]
     return pl.pallas_call(
@@ -433,10 +435,10 @@
     weights = gather_weight(conv_weight, at, n, row)
     pre = None
     for k in PRODUCTS[:2]:
-        pre = product(pre, weights[k].T, [image[m] for m in SETS[k]])
+        pre = product(pre, weights[k], [image[m] for m in SETS[k]])
         pre, params = lax.optimization_barrier((pre, params))
     twin = [exchange(image[m], "mp", n, 1) for m in bit_order(1)]
-    turned = [weights[k].T for k in PRODUCTS[2:]]
+    turned = [weights[k] for k in PRODUCTS[2:]]
     last = [image[m] for k in PRODUCTS[2:] for m in SETS[k]]
     grad_pre, small = head(2 * labels - 1, pre, params, turned, last)
     twin_pre = exchange(grad_pre, "mp", n, 1)

time: 278 us -> 252 us (0.906)
  local copies, waits for them, and re-layouts: 40.7 us -> 7.36 us
  waiting for transfers between devices: 133 us -> 144 us
    unnamed x86 -> x10, local copies, waits for them, and re-layouts: 30 us -> 3.7 us
    ppermute x54, waiting for transfers between devices: 133 us -> 144 us  [exchange(): return lax.ppermute(value, axis, [(i, i ^ mask) for i in range(size)])]
    pallas_call x4 -> x0, local copies, waits for them, and re-layouts: 5.09 us -> none  [local(): pl.pallas_call(kernel, out_shape=outs, in_specs=specs, cost_estimate=pl.C...]
  transfers between devices with their start and end apart: 54 -> 54, of which waited for: 23 -> 26; matrix products, arithmetic and copies ran while one was open for 4% -> 2% of each run, Pallas kernels for 7% -> 7%
where the time goes in v3:
time: 252 us; the launch traced here: 251 us
  waiting for transfers between devices  144 us (57%)
  starting transfers between devices  64.6 us (26%)
  Pallas kernels  32.8 us (13%)
  local copies, waits for them, and re-layouts  7.36 us (3%)
    ppermute x54, waiting for transfers between devices, exchange(): return lax.ppermute(value, axis, [(i, i ^ mask) for i in range(size)])  144 us
    ppermute x54, starting transfers between devices, exchange(): return lax.ppermute(value, axis, [(i, i ^ mask) for i in range(size)])  64.6 us
    pallas_call x10, Pallas kernels, local(): pl.pallas_call(kernel, out_shape=outs, in_specs=specs, cost_estimate=pl.C...  13.3 us
    pallas_call x1, Pallas kernels, head(): pl.pallas_call(head_kernel, out_shape=(jax.ShapeDtypeStruct((ch, cells),...  10.4 us
  transfers between devices with their start and end apart: 54, of which 26 were waited for; matrix products, arithmetic and copies ran while one was open for 2% of the time, Pallas kernels for 7%

profile of v3, /device:TPU:12, one launch (start us, length us, event | category | flops | bytes accessed | tf_op | source)
XLA Modules:
  0.0 251.0 jit_solution(12122171656240007587)
XLA Ops:
  2.2 2.6 %collective-permute-start = (bf16[1,80,640]{2,1,0:T(8,128)(2,1)S(1)}, bf16[1,80,640]{2,1,0:T(8,128)(2,1)S(1)}, u32[]{:S(2)}, u32[]{:S(2)}) collective-permute-start(bf16[1,80,640]{2,1,0:T(8,128)(2,1)S(1)} %get-tuple-element.87), channel_id=1, source_target_pairs={{0,8},{1,9},{2,10},{3,11},{4,12},{5,13},{6,14},{7,15},{8,0},{9,1},... | collective-permute-start | bytes 307208 | tf_op jit(solution)/shard_map/ppermute | solution.py:408
  4.8 4.2 %collective-permute-done = bf16[1,80,640]{2,1,0:T(8,128)(2,1)S(1)} collective-permute-done((bf16[1,80,640]{2,1,0:T(8,128)(2,1)S(1)}, bf16[1,80,640]{2,1,0:T(8,128)(2,1)S(1)}, u32[]{:S(2)}, u32[]{:S(2)}) %collective-permute-start) | collective-permute-done | bytes 102432 | tf_op jit(solution)/shard_map/ppermute | solution.py:408
  10.5 5.6 %collective-permute-done.1 = bf16[2,80,640]{2,1,0:T(8,128)(2,1)S(1)} collective-permute-done((bf16[2,80,640]{2,1,0:T(8,128)(2,1)S(1)}, bf16[2,80,640]{2,1,0:T(8,128)(2,1)S(1)}, u32[]{:S(2)}, u32[]{:S(2)}) %collective-permute-start.1) | collective-permute-done | bytes 204832 | tf_op jit(solution)/shard_map/ppermute | solution.py:408
  17.7 9.0 %collective-permute-done.2 = bf16[4,80,640]{2,1,0:T(8,128)(2,1)S(1)} collective-permute-done((bf16[4,80,640]{2,1,0:T(8,128)(2,1)S(1)}, bf16[4,80,640]{2,1,0:T(8,128)(2,1)S(1)}, u32[]{:S(2)}, u32[]{:S(2)}) %collective-permute-start.2) | collective-permute-done | bytes 409632 | tf_op jit(solution)/shard_map/ppermute | solution.py:408
  29.6 15.8 %collective-permute-done.3.across_ref = bf16[8,80,640]{2,1,0:T(8,128)(2,1)S(1)} collective-permute-done((bf16[8,80,640]{2,1,0:T(8,128)(2,1)S(1)}, bf16[8,80,640]{2,1,0:T(8,128)(2,1)S(1)}, u32[]{:S(2)}, u32[]{:S(2)}) %collective-permute-start.3) | collective-permute-done | bytes 819232 | tf_op jit(solution)/shard_map/ppermute | solution.py:408
  48.5 2.8 %collective-permute-start.5 = (bf16[80,1024]{1,0:T(8,128)(2,1)S(1)}, bf16[80,1024]{1,0:T(8,128)(2,1)S(1)}, u32[]{:S(2)}, u32[]{:S(2)}) collective-permute-start(bf16[80,1024]{1,0:T(8,128)(2,1)S(1)} %get-tuple-element.102), channel_id=1, source_target_pairs={{0,12},{1,13},{2,14},{3,15},{4,8},{5,9},{6,10},{7,11},{8,4},{9,5},... | collective-permute-start | bytes 491528 | tf_op jit(solution)/shard_map/ppermute | solution.py:408
  52.0 2.4 collective-permute-start.7
  55.5 14.9 %collective-permute-done.5.refs_0_.refs_6_ = bf16[80,1024]{1,0:T(8,128)(2,1)S(1)} collective-permute-done((bf16[80,1024]{1,0:T(8,128)(2,1)S(1)}, bf16[80,1024]{1,0:T(8,128)(2,1)S(1)}, u32[]{:S(2)}, u32[]{:S(2)}) %collective-permute-start.5) | collective-permute-done | bytes 163872 | tf_op jit(solution)/shard_map/ppermute | solution.py:408
  70.4 3.1 %collective-permute-done.6.refs_1_.refs_4_ = bf16[80,1024]{1,0:T(8,128)(2,1)S(1)} collective-permute-done((bf16[80,1024]{1,0:T(8,128)(2,1)S(1)}, bf16[80,1024]{1,0:T(8,128)(2,1)S(1)}, u32[]{:S(2)}, u32[]{:S(2)}) %collective-permute-start.6) | collective-permute-done | bytes 163872 | tf_op jit(solution)/shard_map/ppermute | solution.py:408
  73.6 3.5 %collective-permute-done.7.refs_2_ = bf16[80,1024]{1,0:T(8,128)(2,1)S(1)} collective-permute-done((bf16[80,1024]{1,0:T(8,128)(2,1)S(1)}, bf16[80,1024]{1,0:T(8,128)(2,1)S(1)}, u32[]{:S(2)}, u32[]{:S(2)}) %collective-permute-start.7) | collective-permute-done | bytes 163872 | tf_op jit(solution)/shard_map/ppermute | solution.py:408
  77.0 3.0 %collective-permute-done.8.refs_3_ = bf16[80,1024]{1,0:T(8,128)(2,1)S(1)} collective-permute-done((bf16[80,1024]{1,0:T(8,128)(2,1)S(1)}, bf16[80,1024]{1,0:T(8,128)(2,1)S(1)}, u32[]{:S(2)}, u32[]{:S(2)}) %collective-permute-start.8) | collective-permute-done | bytes 163872 | tf_op jit(solution)/shard_map/ppermute | solution.py:408
  81.3 4.1 %collective-permute-start.13 = (bf16[80,1024]{1,0:T(8,128)(2,1)S(1)}, bf16[80,1024]{1,0:T(8,128)(2,1)S(1)}, u32[]{:S(2)}, u32[]{:S(2)}) collective-permute-start(bf16[80,1024]{1,0:T(8,128)(2,1)S(1)} %get-tuple-element.93), channel_id=1, source_target_pairs={{0,10},{1,11},{2,8},{3,9},{4,14},{5,15},{6,12},{7,13},{8,2},{9,3},... | collective-permute-start | bytes 491528 | tf_op jit(solution)/shard_map/ppermute | solution.py:408
  87.0 7.3 %collective-permute-done.12.refs_0_.refs_7_ = bf16[80,1024]{1,0:T(8,128)(2,1)S(1)} collective-permute-done((bf16[80,1024]{1,0:T(8,128)(2,1)S(1)}, bf16[80,1024]{1,0:T(8,128)(2,1)S(1)}, u32[]{:S(2)}, u32[]{:S(2)}) %collective-permute-start.12) | collective-permute-done | bytes 163872 | tf_op jit(solution)/shard_map/ppermute | solution.py:408
  94.3 5.1 %collective-permute-done.13.refs_1_.refs_5_ = bf16[80,1024]{1,0:T(8,128)(2,1)S(1)} collective-permute-done((bf16[80,1024]{1,0:T(8,128)(2,1)S(1)}, bf16[80,1024]{1,0:T(8,128)(2,1)S(1)}, u32[]{:S(2)}, u32[]{:S(2)}) %collective-permute-start.13) | collective-permute-done | bytes 163872 | tf_op jit(solution)/shard_map/ppermute | solution.py:408
  99.4 3.8 %collective-permute-start.17 = (bf16[80,1024]{1,0:T(8,128)(2,1)S(1)}, bf16[80,1024]{1,0:T(8,128)(2,1)S(1)}, u32[]{:S(2)}, u32[]{:S(2)}) collective-permute-start(bf16[80,1024]{1,0:T(8,128)(2,1)S(1)} %get-tuple-element.89), channel_id=1, source_target_pairs={{0,11},{1,10},{2,9},{3,8},{4,15},{5,14},{6,13},{7,12},{8,3},{9,2},... | collective-permute-start | bytes 491528 | tf_op jit(solution)/shard_map/ppermute | solution.py:408
  103.7 2.4 collective-permute-start.19
  112.0 2.8 %collective-permute-done.19.refs_7_ = bf16[80,1024]{1,0:T(8,128)(2,1)S(1)} collective-permute-done((bf16[80,1024]{1,0:T(8,128)(2,1)S(1)}, bf16[80,1024]{1,0:T(8,128)(2,1)S(1)}, u32[]{:S(2)}, u32[]{:S(2)}) %collective-permute-start.19) | collective-permute-done | bytes 163872 | tf_op jit(solution)/shard_map/ppermute | solution.py:408
  114.7 10.4 %head.1 = (bf16[1280,1024]{1,0:T(8,128)(2,1)S(1)}, f32[8,1280]{1,0:T(8,128)S(1)}) custom-call(s32[1]{0:T(128)S(6)} %sub.3.info_ref, f32[1280,1024]{1,0:T(8,128)S(1)} %product.3.begun_ref, f32[3,1280,128]{2,1,0:T(8,128)S(1)} %broadcast_in_dim.10.par_ref, bf16[320,1280]{1,0:T(8,128)(2,1)S(1)} %get-tuple-element.52.weight_ref, ...), custom_call_target="tpu_custom_call" | custom-call | flops 5033164800 | bytes 10485760 | tf_op jit(solution)/shard_map/head/pallas_call | solution.py:140
  126.3 4.0 %collective-permute-done.39.refs_0_ = bf16[80,1024]{1,0:T(8,128)(2,1)S(1)} collective-permute-done((bf16[80,1024]{1,0:T(8,128)(2,1)S(1)}, bf16[80,1024]{1,0:T(8,128)(2,1)S(1)}, u32[]{:S(2)}, u32[]{:S(2)}) %collective-permute-start.39) | collective-permute-done | bytes 163872 | tf_op jit(solution)/shard_map/ppermute | solution.py:408
  133.8 2.6 %shard_map.97 = (f32[328,640]{1,0:T(8,128)S(1)}, f32[328,640]{1,0:T(8,128)S(1)}, f32[320,640]{1,0:T(8,128)S(1)}, f32[320,640]{1,0:T(8,128)S(1)}) custom-call(s32[2]{0:T(128)S(1)} %pad_add_fusion.at_ref, f32[640,1280]{1,0:T(8,128)S(1)} %weight_keep.1.own_ref, bf16[1280,1024]{1,0:T(8,128)(2,1)S(1)} %collective-permute-done.37.pre_grad_ref, ...), custom_call_target="tpu_custom_call" | custom-call | flops 2097152 | bytes 1048576 | tf_op jit(solution)/shard_map/pallas_call | solution.py:259
  138.2 19.1 %collective-permute-done.48.qb = f32[320,640]{1,0:T(8,128)S(1)} collective-permute-done((f32[320,640]{1,0:T(8,128)S(1)}, f32[320,640]{1,0:T(8,128)S(1)}, u32[]{:S(2)}, u32[]{:S(2)}) %collective-permute-start.48) | collective-permute-done | bytes 819232 | tf_op jit(solution)/shard_map/ppermute | solution.py:408
  160.6 9.2 %collective-permute-done.50.qb = f32[160,640]{1,0:T(8,128)S(1)} collective-permute-done((f32[160,640]{1,0:T(8,128)S(1)}, f32[160,640]{1,0:T(8,128)S(1)}, u32[]{:S(2)}, u32[]{:S(2)}) %collective-permute-start.50) | collective-permute-done | bytes 409632 | tf_op jit(solution)/shard_map/ppermute | solution.py:408
  170.5 2.2 collective-permute-start.51
  176.2 3.2 %collective-permute-start.36 = (bf16[80,1024]{1,0:T(8,128)(2,1)S(1)}, bf16[80,1024]{1,0:T(8,128)(2,1)S(1)}, u32[]{:S(2)}, u32[]{:S(2)}) collective-permute-start(bf16[80,1024]{1,0:T(8,128)(2,1)S(1)} %get-tuple-element.69), channel_id=1, source_target_pairs={{0,9},{1,8},{2,11},{3,10},{4,13},{5,12},{6,15},{7,14},{8,1},{9,0},... | collective-permute-start | bytes 491528 | tf_op jit(solution)/shard_map/ppermute | solution.py:408
  182.4 8.0 %collective-permute-start.26 = (bf16[80,1024]{1,0:T(8,128)(2,1)S(1)}, bf16[80,1024]{1,0:T(8,128)(2,1)S(1)}, u32[]{:S(2)}, u32[]{:S(2)}) collective-permute-start(bf16[80,1024]{1,0:T(8,128)(2,1)S(1)} %get-tuple-element.60), channel_id=1, source_target_pairs={{0,4},{1,5},{2,6},{3,7},{4,0},{5,1},{6,2},{7,3},{8,12},{9,13},{10,... | collective-permute-start | bytes 491528 | tf_op jit(solution)/shard_map/ppermute | solution.py:408
  190.3 7.6 %collective-permute-done.34.refs_2_ = bf16[80,1024]{1,0:T(8,128)(2,1)S(1)} collective-permute-done((bf16[80,1024]{1,0:T(8,128)(2,1)S(1)}, bf16[80,1024]{1,0:T(8,128)(2,1)S(1)}, u32[]{:S(2)}, u32[]{:S(2)}) %collective-permute-start.34) | collective-permute-done | bytes 163872 | tf_op jit(solution)/shard_map/ppermute | solution.py:408
  198.0 2.4 collective-permute-done.35.refs_3_
  205.2 2.5 collective-permute-start.52
  208.6 13.3 %collective-permute-done.29 = bf16[80,1024]{1,0:T(8,128)(2,1)S(1)} collective-permute-done((bf16[80,1024]{1,0:T(8,128)(2,1)S(1)}, bf16[80,1024]{1,0:T(8,128)(2,1)S(1)}, u32[]{:S(2)}, u32[]{:S(2)}) %collective-permute-start.29) | collective-permute-done | bytes 163872 | tf_op jit(solution)/shard_map/ppermute | solution.py:408
  226.3 5.6 %collective-permute-start.21 = (bf16[80,1024]{1,0:T(8,128)(2,1)S(1)}, bf16[80,1024]{1,0:T(8,128)(2,1)S(1)}, u32[]{:S(2)}, u32[]{:S(2)}) collective-permute-start(bf16[80,1024]{1,0:T(8,128)(2,1)S(1)} %get-tuple-element.55), channel_id=1, source_target_pairs={{0,11},{1,10},{2,9},{3,8},{4,15},{5,14},{6,13},{7,12},{8,3},{9,2},... | collective-permute-start | bytes 491528 | tf_op jit(solution)/shard_map/ppermute | solution.py:408
  238.0 5.8 %collective-permute-done.20.refs_0_ = bf16[80,1024]{1,0:T(8,128)(2,1)S(1)} collective-permute-done((bf16[80,1024]{1,0:T(8,128)(2,1)S(1)}, bf16[80,1024]{1,0:T(8,128)(2,1)S(1)}, u32[]{:S(2)}, u32[]{:S(2)}) %collective-permute-start.20) | collective-permute-done | bytes 163872 | tf_op jit(solution)/shard_map/ppermute | solution.py:408
  244.8 2.9 %collective-permute-done.23.refs_3_ = bf16[80,1024]{1,0:T(8,128)(2,1)S(1)} collective-permute-done((bf16[80,1024]{1,0:T(8,128)(2,1)S(1)}, bf16[80,1024]{1,0:T(8,128)(2,1)S(1)}, u32[]{:S(2)}, u32[]{:S(2)}) %collective-permute-start.23) | collective-permute-done | bytes 163872 | tf_op jit(solution)/shard_map/ppermute | solution.py:408
  (115 shorter events, 58.1 us)
Async XLA Ops:
  26.9 18.5 %collective-permute-start.3 = (bf16[8,80,640]{2,1,0:T(8,128)(2,1)S(1)}, bf16[8,80,640]{2,1,0:T(8,128)(2,1)S(1)}, u32[]{:S(2)}, u32[]{:S(2)}) collective-permute-start(bf16[8,80,640]{2,1,0:T(8,128)(2,1)S(1)} %pad_maximum_fusion.near_ref), channel_id=1, source_target_pairs={{0,16},{16,0},{1,17},{17,1},{2,18},{18,2},{3,19},{19,3},{4,20},{20... | collective-permute-start | bytes 2457608 | tf_op jit(solution)/shard_map/ppermute | solution.py:408
  46.3 57.3 %collective-permute-start.4 = (bf16[16,80,640]{2,1,0:T(8,128)(2,1)}, bf16[16,80,640]{2,1,0:T(8,128)(2,1)S(1)}, u32[]{:S(2)}, u32[]{:S(2)}) collective-permute-start(bf16[16,80,640]{2,1,0:T(8,128)(2,1)} %constant_dynamic-update-slice_fusion), channel_id=1, source_target_pairs={{0,1},{1,0},{2,3},{3,2},{4,5},{5,4},{6,7},{7,6},{8,9},{9,8},{10,11... | collective-permute-start | bytes 4915208 | tf_op jit(solution)/shard_map/ppermute | solution.py:408
  48.5 21.9 %collective-permute-start.5 = (bf16[80,1024]{1,0:T(8,128)(2,1)S(1)}, bf16[80,1024]{1,0:T(8,128)(2,1)S(1)}, u32[]{:S(2)}, u32[]{:S(2)}) collective-permute-start(bf16[80,1024]{1,0:T(8,128)(2,1)S(1)} %get-tuple-element.102), channel_id=1, source_target_pairs={{0,12},{1,13},{2,14},{3,15},{4,8},{5,9},{6,10},{7,11},{8,4},{9,5},... | collective-permute-start | bytes 491528 | tf_op jit(solution)/shard_map/ppermute | solution.py:408
  51.3 22.2 %collective-permute-start.6 = (bf16[80,1024]{1,0:T(8,128)(2,1)S(1)}, bf16[80,1024]{1,0:T(8,128)(2,1)S(1)}, u32[]{:S(2)}, u32[]{:S(2)}) collective-permute-start(bf16[80,1024]{1,0:T(8,128)(2,1)S(1)} %get-tuple-element.101), channel_id=1, source_target_pairs={{0,8},{1,9},{2,10},{3,11},{4,12},{5,13},{6,14},{7,15},{8,0},{9,1},... | collective-permute-start | bytes 491528 | tf_op jit(solution)/shard_map/ppermute | solution.py:408
  52.0 25.0 %collective-permute-start.7 = (bf16[80,1024]{1,0:T(8,128)(2,1)S(1)}, bf16[80,1024]{1,0:T(8,128)(2,1)S(1)}, u32[]{:S(2)}, u32[]{:S(2)}) collective-permute-start(bf16[80,1024]{1,0:T(8,128)(2,1)S(1)} %get-tuple-element.100), channel_id=1, source_target_pairs={{0,13},{1,12},{2,15},{3,14},{4,9},{5,8},{6,11},{7,10},{8,5},{9,4},... | collective-permute-start | bytes 491528 | tf_op jit(solution)/shard_map/ppermute | solution.py:408
  54.4 25.7 %collective-permute-start.8 = (bf16[80,1024]{1,0:T(8,128)(2,1)S(1)}, bf16[80,1024]{1,0:T(8,128)(2,1)S(1)}, u32[]{:S(2)}, u32[]{:S(2)}) collective-permute-start(bf16[80,1024]{1,0:T(8,128)(2,1)S(1)} %get-tuple-element.99), channel_id=1, source_target_pairs={{0,9},{1,8},{2,11},{3,10},{4,13},{5,12},{6,15},{7,14},{8,1},{9,0},... | collective-permute-start | bytes 491528 | tf_op jit(solution)/shard_map/ppermute | solution.py:408
  73.5 11.9 %collective-permute-start.11 = (bf16[80,1024]{1,0:T(8,128)(2,1)S(1)}, bf16[80,1024]{1,0:T(8,128)(2,1)S(1)}, u32[]{:S(2)}, u32[]{:S(2)}) collective-permute-start(bf16[80,1024]{1,0:T(8,128)(2,1)S(1)} %get-tuple-element.96), channel_id=1, source_target_pairs={{0,1},{1,0},{2,3},{3,2},{4,5},{5,4},{6,7},{7,6},{8,9},{9,8},{10,11... | collective-permute-start | bytes 491528 | tf_op jit(solution)/shard_map/ppermute | solution.py:408
  80.1 14.2 %collective-permute-start.12 = (bf16[80,1024]{1,0:T(8,128)(2,1)S(1)}, bf16[80,1024]{1,0:T(8,128)(2,1)S(1)}, u32[]{:S(2)}, u32[]{:S(2)}) collective-permute-start(bf16[80,1024]{1,0:T(8,128)(2,1)S(1)} %get-tuple-element.94), channel_id=1, source_target_pairs={{0,14},{1,15},{2,12},{3,13},{4,10},{5,11},{6,8},{7,9},{8,6},{9,7},... | collective-permute-start | bytes 491528 | tf_op jit(solution)/shard_map/ppermute | solution.py:408
  81.3 18.1 %collective-permute-start.13 = (bf16[80,1024]{1,0:T(8,128)(2,1)S(1)}, bf16[80,1024]{1,0:T(8,128)(2,1)S(1)}, u32[]{:S(2)}, u32[]{:S(2)}) collective-permute-start(bf16[80,1024]{1,0:T(8,128)(2,1)S(1)} %get-tuple-element.93), channel_id=1, source_target_pairs={{0,10},{1,11},{2,8},{3,9},{4,14},{5,15},{6,12},{7,13},{8,2},{9,3},... | collective-permute-start | bytes 491528 | tf_op jit(solution)/shard_map/ppermute | solution.py:408
  85.4 17.8 %collective-permute-start.14 = (bf16[80,1024]{1,0:T(8,128)(2,1)S(1)}, bf16[80,1024]{1,0:T(8,128)(2,1)S(1)}, u32[]{:S(2)}, u32[]{:S(2)}) collective-permute-start(bf16[80,1024]{1,0:T(8,128)(2,1)S(1)} %get-tuple-element.92), channel_id=1, source_target_pairs={{0,2},{1,3},{2,0},{3,1},{4,6},{5,7},{6,4},{7,5},{8,10},{9,11},{10,... | collective-permute-start | bytes 491528 | tf_op jit(solution)/shard_map/ppermute | solution.py:408
  86.9 24.5 %collective-permute-start.15 = (bf16[80,1024]{1,0:T(8,128)(2,1)S(1)}, bf16[80,1024]{1,0:T(8,128)(2,1)S(1)}, u32[]{:S(2)}, u32[]{:S(2)}) collective-permute-start(bf16[80,1024]{1,0:T(8,128)(2,1)S(1)} %get-tuple-element.91), channel_id=1, source_target_pairs={{0,3},{1,2},{2,1},{3,0},{4,7},{5,6},{6,5},{7,4},{8,11},{9,10},{10,... | collective-permute-start | bytes 491528 | tf_op jit(solution)/shard_map/ppermute | solution.py:408
  94.3 17.2 %collective-permute-start.16 = (bf16[80,1024]{1,0:T(8,128)(2,1)S(1)}, bf16[80,1024]{1,0:T(8,128)(2,1)S(1)}, u32[]{:S(2)}, u32[]{:S(2)}) collective-permute-start(bf16[80,1024]{1,0:T(8,128)(2,1)S(1)} %get-tuple-element.90), channel_id=1, source_target_pairs={{0,15},{1,14},{2,13},{3,12},{4,11},{5,10},{6,9},{7,8},{8,7},{9,6},... | collective-permute-start | bytes 491528 | tf_op jit(solution)/shard_map/ppermute | solution.py:408
  99.4 12.0 %collective-permute-start.17 = (bf16[80,1024]{1,0:T(8,128)(2,1)S(1)}, bf16[80,1024]{1,0:T(8,128)(2,1)S(1)}, u32[]{:S(2)}, u32[]{:S(2)}) collective-permute-start(bf16[80,1024]{1,0:T(8,128)(2,1)S(1)} %get-tuple-element.89), channel_id=1, source_target_pairs={{0,11},{1,10},{2,9},{3,8},{4,15},{5,14},{6,13},{7,12},{8,3},{9,2},... | collective-permute-start | bytes 491528 | tf_op jit(solution)/shard_map/ppermute | solution.py:408
  103.7 11.1 %collective-permute-start.19 = (bf16[80,1024]{1,0:T(8,128)(2,1)S(1)}, bf16[80,1024]{1,0:T(8,128)(2,1)S(1)}, u32[]{:S(2)}, u32[]{:S(2)}) collective-permute-start(bf16[80,1024]{1,0:T(8,128)(2,1)S(1)} %get-tuple-element.88), channel_id=1, source_target_pairs={{0,7},{1,6},{2,5},{3,4},{4,3},{5,2},{6,1},{7,0},{8,15},{9,14},{10,... | collective-permute-start | bytes 491528 | tf_op jit(solution)/shard_map/ppermute | solution.py:408
  136.5 21.0 %collective-permute-start.47 = (f32[328,640]{1,0:T(8,128)S(1)}, f32[328,640]{1,0:T(8,128)S(1)}, u32[]{:S(2)}, u32[]{:S(2)}) collective-permute-start(f32[328,640]{1,0:T(8,128)S(1)} %get-tuple-element.72), channel_id=1, source_target_pairs={{0,16},{16,0},{1,17},{17,1},{2,18},{18,2},{3,19},{19,3},{4,20},{20... | collective-permute-start | bytes 2519048 | tf_op jit(solution)/shard_map/ppermute | solution.py:408
  137.0 20.3 %collective-permute-start.48 = (f32[320,640]{1,0:T(8,128)S(1)}, f32[320,640]{1,0:T(8,128)S(1)}, u32[]{:S(2)}, u32[]{:S(2)}) collective-permute-start(f32[320,640]{1,0:T(8,128)S(1)} %get-tuple-element.74), channel_id=1, source_target_pairs={{0,2},{1,3},{2,0},{3,1},{4,6},{5,7},{6,4},{7,5},{8,10},{9,11},{10,... | collective-permute-start | bytes 2457608 | tf_op jit(solution)/shard_map/ppermute | solution.py:408
  158.2 11.6 %collective-permute-start.49 = (f32[168,640]{1,0:T(8,128)S(1)}, f32[168,640]{1,0:T(8,128)S(1)}, u32[]{:S(2)}, u32[]{:S(2)}) collective-permute-start(f32[168,640]{1,0:T(8,128)S(1)} %get-tuple-element.76), channel_id=1, source_target_pairs={{0,2},{1,3},{2,0},{3,1},{4,6},{5,7},{6,4},{7,5},{8,10},{9,11},{10,... | collective-permute-start | bytes 1290248 | tf_op jit(solution)/shard_map/ppermute | solution.py:408
  170.5 33.6 %collective-permute-start.51 = (f32[88,1280]{1,0:T(8,128)S(1)}, f32[88,1280]{1,0:T(8,128)S(1)}, u32[]{:S(2)}, u32[]{:S(2)}) collective-permute-start(f32[88,1280]{1,0:T(8,128)S(1)} %get-tuple-element.80), channel_id=1, source_target_pairs={{0,4},{1,5},{2,6},{3,7},{4,0},{5,1},{6,2},{7,3},{8,12},{9,13},{10,... | collective-permute-start | bytes 1351688 | tf_op jit(solution)/shard_map/ppermute | solution.py:408
  175.7 22.2 %collective-permute-start.34 = (bf16[80,1024]{1,0:T(8,128)(2,1)S(1)}, bf16[80,1024]{1,0:T(8,128)(2,1)S(1)}, u32[]{:S(2)}, u32[]{:S(2)}) collective-permute-start(bf16[80,1024]{1,0:T(8,128)(2,1)S(1)} %get-tuple-element.67), channel_id=1, source_target_pairs={{0,8},{1,9},{2,10},{3,11},{4,12},{5,13},{6,14},{7,15},{8,0},{9,1},... | collective-permute-start | bytes 491528 | tf_op jit(solution)/shard_map/ppermute | solution.py:408
  176.1 24.2 %collective-permute-start.35 = (bf16[80,1024]{1,0:T(8,128)(2,1)S(1)}, bf16[80,1024]{1,0:T(8,128)(2,1)S(1)}, u32[]{:S(2)}, u32[]{:S(2)}) collective-permute-start(bf16[80,1024]{1,0:T(8,128)(2,1)S(1)} %get-tuple-element.68), channel_id=1, source_target_pairs={{0,13},{1,12},{2,15},{3,14},{4,9},{5,8},{6,11},{7,10},{8,5},{9,4},... | collective-permute-start | bytes 491528 | tf_op jit(solution)/shard_map/ppermute | solution.py:408
  176.2 26.3 %collective-permute-start.36 = (bf16[80,1024]{1,0:T(8,128)(2,1)S(1)}, bf16[80,1024]{1,0:T(8,128)(2,1)S(1)}, u32[]{:S(2)}, u32[]{:S(2)}) collective-permute-start(bf16[80,1024]{1,0:T(8,128)(2,1)S(1)} %get-tuple-element.69), channel_id=1, source_target_pairs={{0,9},{1,8},{2,11},{3,10},{4,13},{5,12},{6,15},{7,14},{8,1},{9,0},... | collective-permute-start | bytes 491528 | tf_op jit(solution)/shard_map/ppermute | solution.py:408
  182.4 22.8 %collective-permute-start.26 = (bf16[80,1024]{1,0:T(8,128)(2,1)S(1)}, bf16[80,1024]{1,0:T(8,128)(2,1)S(1)}, u32[]{:S(2)}, u32[]{:S(2)}) collective-permute-start(bf16[80,1024]{1,0:T(8,128)(2,1)S(1)} %get-tuple-element.60), channel_id=1, source_target_pairs={{0,4},{1,5},{2,6},{3,7},{4,0},{5,1},{6,2},{7,3},{8,12},{9,13},{10,... | collective-permute-start | bytes 491528 | tf_op jit(solution)/shard_map/ppermute | solution.py:408
  202.5 19.4 %collective-permute-start.29 = (bf16[80,1024]{1,0:T(8,128)(2,1)S(1)}, bf16[80,1024]{1,0:T(8,128)(2,1)S(1)}, u32[]{:S(2)}, u32[]{:S(2)}) collective-permute-start(bf16[80,1024]{1,0:T(8,128)(2,1)S(1)} %get-tuple-element.63), channel_id=1, source_target_pairs={{0,12},{1,13},{2,14},{3,15},{4,8},{5,9},{6,10},{7,11},{8,4},{9,5},... | collective-permute-start | bytes 491528 | tf_op jit(solution)/shard_map/ppermute | solution.py:408
  204.1 20.0 %collective-permute-start.31 = (bf16[80,1024]{1,0:T(8,128)(2,1)S(1)}, bf16[80,1024]{1,0:T(8,128)(2,1)S(1)}, u32[]{:S(2)}, u32[]{:S(2)}) collective-permute-start(bf16[80,1024]{1,0:T(8,128)(2,1)S(1)} %get-tuple-element.64), channel_id=1, source_target_pairs={{0,8},{1,9},{2,10},{3,11},{4,12},{5,13},{6,14},{7,15},{8,0},{9,1},... | collective-permute-start | bytes 491528 | tf_op jit(solution)/shard_map/ppermute | solution.py:408
  205.2 26.8 %collective-permute-start.52 = (f32[48,1280]{1,0:T(8,128)S(1)}, f32[48,1280]{1,0:T(8,128)S(1)}, u32[]{:S(2)}, u32[]{:S(2)}) collective-permute-start(f32[48,1280]{1,0:T(8,128)S(1)} %get-tuple-element.82), channel_id=1, source_target_pairs={{0,8},{1,9},{2,10},{3,11},{4,12},{5,13},{6,14},{7,15},{8,0},{9,1},... | collective-permute-start | bytes 737288 | tf_op jit(solution)/shard_map/ppermute | solution.py:408
  207.7 18.6 %collective-permute-start.24 = (bf16[80,1024]{1,0:T(8,128)(2,1)S(1)}, bf16[80,1024]{1,0:T(8,128)(2,1)S(1)}, u32[]{:S(2)}, u32[]{:S(2)}) collective-permute-start(bf16[80,1024]{1,0:T(8,128)(2,1)S(1)} %get-tuple-element.58), channel_id=1, source_target_pairs={{0,2},{1,3},{2,0},{3,1},{4,6},{5,7},{6,4},{7,5},{8,10},{9,11},{10,... | collective-permute-start | bytes 491528 | tf_op jit(solution)/shard_map/ppermute | solution.py:408
  208.6 17.7 %collective-permute-start.25 = (bf16[80,1024]{1,0:T(8,128)(2,1)S(1)}, bf16[80,1024]{1,0:T(8,128)(2,1)S(1)}, u32[]{:S(2)}, u32[]{:S(2)}) collective-permute-start(bf16[80,1024]{1,0:T(8,128)(2,1)S(1)} %get-tuple-element.59), channel_id=1, source_target_pairs={{0,3},{1,2},{2,1},{3,0},{4,7},{5,6},{6,5},{7,4},{8,11},{9,10},{10,... | collective-permute-start | bytes 491528 | tf_op jit(solution)/shard_map/ppermute | solution.py:408
  226.3 17.6 %collective-permute-start.20 = (bf16[80,1024]{1,0:T(8,128)(2,1)S(1)}, bf16[80,1024]{1,0:T(8,128)(2,1)S(1)}, u32[]{:S(2)}, u32[]{:S(2)}) collective-permute-start(bf16[80,1024]{1,0:T(8,128)(2,1)S(1)} %get-tuple-element.54), channel_id=1, source_target_pairs={{0,15},{1,14},{2,13},{3,12},{4,11},{5,10},{6,9},{7,8},{8,7},{9,6},... | collective-permute-start | bytes 491528 | tf_op jit(solution)/shard_map/ppermute | solution.py:408
  226.3 18.5 %collective-permute-start.21 = (bf16[80,1024]{1,0:T(8,128)(2,1)S(1)}, bf16[80,1024]{1,0:T(8,128)(2,1)S(1)}, u32[]{:S(2)}, u32[]{:S(2)}) collective-permute-start(bf16[80,1024]{1,0:T(8,128)(2,1)S(1)} %get-tuple-element.55), channel_id=1, source_target_pairs={{0,11},{1,10},{2,9},{3,8},{4,15},{5,14},{6,13},{7,12},{8,3},{9,2},... | collective-permute-start | bytes 491528 | tf_op jit(solution)/shard_map/ppermute | solution.py:408
  231.9 12.9 %collective-permute-start.22 = (bf16[80,1024]{1,0:T(8,128)(2,1)S(1)}, bf16[80,1024]{1,0:T(8,128)(2,1)S(1)}, u32[]{:S(2)}, u32[]{:S(2)}) collective-permute-start(bf16[80,1024]{1,0:T(8,128)(2,1)S(1)} %get-tuple-element.56), channel_id=1, source_target_pairs={{0,6},{1,7},{2,4},{3,5},{4,2},{5,3},{6,0},{7,1},{8,14},{9,15},{10,... | collective-permute-start | bytes 491528 | tf_op jit(solution)/shard_map/ppermute | solution.py:408
  232.0 15.8 %collective-permute-start.23 = (bf16[80,1024]{1,0:T(8,128)(2,1)S(1)}, bf16[80,1024]{1,0:T(8,128)(2,1)S(1)}, u32[]{:S(2)}, u32[]{:S(2)}) collective-permute-start(bf16[80,1024]{1,0:T(8,128)(2,1)S(1)} %get-tuple-element.57), channel_id=1, source_target_pairs={{0,7},{1,6},{2,5},{3,4},{4,3},{5,2},{6,1},{7,0},{8,15},{9,14},{10,... | collective-permute-start | bytes 491528 | tf_op jit(solution)/shard_map/ppermute | solution.py:408
  233.7 16.0 %collective-permute-start.53 = (bf16[40,1280]{1,0:T(8,128)(2,1)S(1)}, bf16[40,1280]{1,0:T(8,128)(2,1)S(1)}, u32[]{:S(2)}, u32[]{:S(2)}) collective-permute-start(bf16[40,1280]{1,0:T(8,128)(2,1)S(1)} %get-tuple-element.83.part), channel_id=1, source_target_pairs={{0,16},{16,0},{1,17},{17,1},{2,18},{18,2},{3,19},{19,3},{4,20},{20... | collective-permute-start | bytes 307208 | tf_op jit(solution)/shard_map/ppermute | solution.py:408
  (25 other events, 233.1 us)
